TPU v7x, 256 devices: a whole 4x4x8 slice. The times are simulated.
256 devices in a mesh: seq: 32 (over y, x, core), tp: 8 (over z).
Axes of the slice: x: 4, y: 4, z: 8, core: 2. Of those that a mesh axis runs over, the one named last changes fastest.
Arguments:
- hidden_in: bfloat16 [2, 16384, 2560], P(None, 'seq'), may hold values from -6 to 6
- gate_proj: bfloat16 [2560, 5120], P(None, 'tp'), may hold values from -0.125 to 0.125
- value_proj: bfloat16 [2560, 5120], P(None, 'tp'), may hold values from -0.125 to 0.125
- bc_proj: bfloat16 [2560, 256], P(None, 'tp'), may hold values from -0.125 to 0.125
- step_proj: bfloat16 [2560, 80], P(None, 'tp'), may hold values from -0.125 to 0.125
- value_conv: float32 [4, 5120], P(None, 'tp'), may hold values from -3 to 3
- bc_conv: float32 [4, 256], replicated, may hold values from -3 to 3
- step_bias: float32 [80], P('tp'), may hold values from -1.5 to 0
- log_rate: float32 [80], P('tp'), as said below
- norm_gain: float32 [5120], P('tp'), may hold values from 0.25 to 1.75
Outputs:
- mixer_out: bfloat16 [2, 16384, 5120], P(None, 'seq', 'tp')
Inputs may be any that keep to these rules, and one draw needn't show every extreme that they name: log_rate lies between -1.5 - ln(16384) and 1.0 - ln(16384).
All inputs are finite; a program needn't handle non-finite values.
Results may differ from a plain program's by a relative error of at most 0.0095.
Values may be sent and summed in bfloat16 or wider, within the bound.
A program may use at most 128 MiB of HBM per device.

v0:
```python
import jax
import jax.numpy as jnp
from jax import lax
from jax.sharding import Mesh
from jax.sharding import PartitionSpec as P

DI = 5120
HEAD_DIM = 64
STATE = 128
CONV = 4
BLOCK = 64
SEQ = ("seq_0", "seq_1", "seq_2")


epsilon = 1e-05


def passed_along(block, axis, distance):
    devices = range(lax.axis_size(axis))
    route = [(i - distance, i) for i in devices if i - distance in devices]
    return lax.ppermute(block, axis, route)


def filled_with(x, identity):
    return jax.tree.map(
        lambda part, zero: jnp.zeros_like(part) + jnp.asarray(zero, part.dtype), x, identity
    )


def entering(x, axes, combine, identity, reverse):
    before = start = filled_with(x, identity)
    so_far = x
    for axis in reversed(axes):
        length, index = lax.axis_size(axis), lax.axis_index(axis)
        pieces = jax.tree.map(lambda part: lax.all_gather(part, axis), so_far)
        inside, so_far = start, start
        for k in reversed(range(length)) if reverse else range(length):
            passed = k > index if reverse else k < index
            so_far = combine(so_far, jax.tree.map(lambda part: part[k], pieces))
            inside = jax.tree.map(lambda new, old: jnp.where(passed, new, old), so_far, inside)
        before = combine(inside, before)
    return before


def conv_silu(padded, kernel, length):
    running = jnp.zeros((padded.shape[0], length, padded.shape[2]), jnp.float32)
    for tap_index in range(kernel.shape[0]):
        running = running + kernel[tap_index] * padded[:, tap_index : tap_index + length, :]
    return jax.nn.silu(running)


def block_step(carried, inputs):
    values, log_decay, step_sizes, b_rows, c_rows = inputs
    length = log_decay.shape[1]
    cumulative = jnp.cumsum(log_decay, axis=1)
    log_gap = cumulative[:, :, None, :] - cumulative[:, None, :, :]
    causal = jnp.arange(length)[:, None] >= jnp.arange(length)[None, :]
    weights_in = jnp.exp(jnp.where(causal[None, :, :, None], log_gap, -jnp.inf))
    scores = jnp.einsum("bin,bjn->bij", c_rows, b_rows, precision=lax.Precision.HIGHEST)
    mixing = scores[:, :, :, None] * weights_in * step_sizes[:, None, :, :]
    within = jnp.einsum("bijh,bjhp->bihp", mixing, values, precision=lax.Precision.HIGHEST)
    earlier = jnp.einsum("bin,bhpn->bihp", c_rows, carried, precision=lax.Precision.HIGHEST)
    earlier = earlier * jnp.exp(cumulative)[..., None]
    remain = jnp.exp(cumulative[:, -1:, :] - cumulative) * step_sizes
    added_state = jnp.einsum(
        "bjh,bjhp,bjn->bhpn", remain, values, b_rows, precision=lax.Precision.HIGHEST
    )
    updated = jnp.exp(cumulative[:, -1, :])[:, :, None, None] * carried + added_state
    return (updated, within + earlier)


def to_blocks(series, batch_size, blocks):
    return jnp.moveaxis(series.reshape((batch_size, blocks, BLOCK) + series.shape[2:]), 1, 0)


def combine(earlier, latter):
    return (earlier[0] * latter[0], latter[0][:, :, None, None] * earlier[1] + latter[1])


def on_device(
    hidden_in,
    gate_proj,
    value_proj,
    bc_proj,
    step_proj,
    value_conv,
    bc_conv,
    step_bias,
    log_rate,
    norm_gain,
):
    batch_size, length, model_width = hidden_in.shape
    heads_here = step_proj.shape[1]
    inner_here = value_proj.shape[1]
    flat_rows = hidden_in.reshape(-1, model_width)
    gate_pre = jnp.dot(flat_rows, gate_proj, preferred_element_type=jnp.float32).astype(
        jnp.bfloat16
    )
    value_pre = jnp.dot(flat_rows, value_proj, preferred_element_type=jnp.float32).astype(
        jnp.bfloat16
    )
    step_pre = jnp.dot(flat_rows, step_proj, preferred_element_type=jnp.float32)
    bc_part = jnp.dot(flat_rows, bc_proj, preferred_element_type=jnp.float32).astype(jnp.bfloat16)
    bc_pre = lax.all_gather(bc_part, "tp", axis=1, tiled=True)
    joined = jnp.concatenate([value_pre, bc_pre], axis=1).reshape(batch_size, length, -1)
    tail_rows = joined[:, length - (CONV - 1) :, :]
    before = passed_along(tail_rows, SEQ, 1)
    padded = jnp.concatenate([before, joined], axis=1).astype(jnp.float32)
    kernel = jnp.concatenate([value_conv, bc_conv], axis=1)
    mixed_in = conv_silu(padded, kernel, length)
    values = mixed_in[..., :inner_here].reshape(batch_size, length, heads_here, HEAD_DIM)
    b_rows = mixed_in[..., inner_here : inner_here + STATE]
    c_rows = mixed_in[..., inner_here + STATE :]
    step_sizes = jax.nn.softplus(step_pre.reshape(batch_size, length, heads_here) + step_bias)
    log_decay = -step_sizes * jnp.exp(log_rate)
    blocks = length // BLOCK
    initial = jnp.zeros((batch_size, heads_here, HEAD_DIM, STATE), jnp.float32)
    local_state, outputs = lax.scan(
        block_step,
        initial,
        (
            to_blocks(values, batch_size, blocks),
            to_blocks(log_decay, batch_size, blocks),
            to_blocks(step_sizes, batch_size, blocks),
            to_blocks(b_rows, batch_size, blocks),
            to_blocks(c_rows, batch_size, blocks),
        ),
    )
    within = jnp.moveaxis(outputs, 0, 1).reshape(batch_size, length, heads_here, HEAD_DIM)
    cumulative = jnp.cumsum(log_decay, axis=1)
    decays = jnp.exp(cumulative[:, -1, :])
    arrived = entering(
        (decays, local_state),
        SEQ,
        combine,
        (jnp.ones_like(decays), jnp.zeros_like(local_state)),
        False,
    )[1]
    correction = jnp.einsum("btn,bhpn->bthp", c_rows, arrived, precision=lax.Precision.HIGHEST)
    correction = correction * jnp.exp(cumulative)[..., None]
    mixed_out = (within + correction).reshape(batch_size, length, inner_here)
    gated_out = mixed_out * jax.nn.silu(
        gate_pre.reshape(batch_size, length, inner_here).astype(jnp.float32)
    )
    squares = jnp.sum(gated_out * gated_out, axis=-1, keepdims=True)
    whole_sq = lax.psum(squares, "tp")
    return (gated_out * lax.rsqrt(whole_sq / DI + epsilon) * norm_gain).astype(jnp.bfloat16)


def solution(mesh):
    split = Mesh(mesh.devices.reshape(4, 4, 2, mesh.shape["tp"]), ("seq_0", "seq_1", "seq_2", "tp"))
    placed = (
        P(None, SEQ, None),
        P(None, "tp"),
        P(None, "tp"),
        P(None, "tp"),
        P(None, "tp"),
        P(None, "tp"),
        P(),
        P("tp"),
        P("tp"),
        P("tp"),
    )
    return jax.shard_map(
        on_device, mesh=split, in_specs=placed, out_specs=P(None, SEQ, "tp"), check_vma=False
    )
```

profile of v0, /device:TPU:1, one launch (start us, length us, event | category | flops | bytes accessed | tf_op | source)
XLA Modules:
  0.0 266.5 jit_solution(15965139563152484885)
XLA Ops:
  8.5 6.2 %convolution_convert_fusion.1 = bf16[1024,640]{0,1:T(8,128)(2,1)S(1)} fusion(bf16[1024,2560]{1,0:T(8,128)(2,1)} %bitcast.229, bf16[2560,640]{1,0:T(8,128)(2,1)S(1)} %copy-done), kind=kOutput, calls=%fused_computation.57 | convolution fusion | flops 3356098560 | bytes 9830400 | tf_op jit(solution)/shard_map/dot_general | solution.py:99
  16.3 23.7 %all_gather.29 = bf16[1024,256]{0,1:T(8,128)(2,1)S(1)} all-gather(bf16[1024,32]{0,1:T(8,128)(2,1)S(1)} %convolution_convert_fusion.2), channel_id=1, replica_groups=mesh['seq_0'=4,'seq_1'=4,'seq_2'=2,'tp'=8] {'tp'}, dimensions={1}, use_global_device_ids=true | all-gather | bytes 589824 | tf_op jit(solution)/shard_map/all_gather | solution.py:104
  41.5 3.1 %copy.121 = bf16[1024,896]{1,0:T(8,128)(2,1)S(1)} copy(bf16[1024,896]{0,1:T(8,128)(2,1)} %pad_maximum_fusion) | data formatting | bytes 3670016 | tf_op jit(solution)/shard_map/reshape | solution.py:105
  44.6 10.1 %collective-permute-start = (bf16[2,3,896]{2,1,0:T(4,128)(2,1)S(1)}, bf16[2,3,896]{2,1,0:T(4,128)(2,1)S(1)}, u32[]{:S(2)}, u32[]{:S(2)}) collective-permute-start(bf16[2,3,896]{2,1,0:T(4,128)(2,1)S(1)} %slice.155), channel_id=1, source_target_pairs={{0,8},{8,16},{16,24},{24,32},{32,40},{40,48},{48,56},{56,64},{64,7... | collective-permute-start | bytes 32264 | tf_op jit(solution)/shard_map/ppermute | solution.py:21
  54.7 4.0 %fusion.102 = (f32[2,10,512]{2,1,0:T(8,128)S(1)}, f32[2,512,10]{1,2,0:T(8,128)S(1)}) fusion(f32[10]{0:T(128)S(1)} %exp.58, f32[10]{0:T(128)S(1)} %copy-done.14, bf16[2,512,2560]{2,1,0:T(8,128)(2,1)} %param.12, bf16[2560,10]{0,1:T(8,128)(2,1)S(1)} %copy-done.10), kind=kOutput, calls=%fused_computation.135 | convolution fusion | flops 52520960 | bytes 5376080 | tf_op jit(solution)/shard_map/dot_general | solution.py:102
  66.2 4.9 %reshape_reshape.3 = f32[2,8,64,10,64]{2,1,4,3,0:T(8,128)} reshape(f32[2,512,640]{1,2,0:T(8,128)} %copy.96) | data formatting | bytes 5242880 | tf_op jit(solution)/shard_map/reshape;reshape | solution.py:73
  71.2 62.0 %while.13 = (s32[]{:T(128)}, f32[2,10,64,128]{3,2,1,0:T(8,128)S(1)}, f32[8,2,64,10,64]{2,4,3,1,0:T(8,128)}, f32[8,2,64,10]{2,0,1,3:T(8,128)S(1)}, f32[8,2,64,10]...) while((s32[]{:T(128)}, ...), condition=%wide.region_2.3_spmd.clone, body=%wide.region_0.2_spmd.clone.sunk | while | flops 328471808 | bytes 6140956 | solution.py:118
  72.7 3.1 %constant_dynamic-slice_fusion.5 = f32[1,2,64,10,64]{2,0,4,3,1:T(1,128)S(1)} fusion(f32[8,2,64,10,64]{2,0,4,3,1:T(8,128)} %get-tuple-element.235, s32[]{:T(128)} %get-tuple-element.219), kind=kLoop, calls=%fused_computation.37.clone.1 | loop fusion | bytes 655364 | tf_op jit(solution)/shard_map/while/body/jit(dynamic_index_in_dim)/dynamic_slice | solution.py:118
  80.5 3.1 %constant_dynamic-slice_fusion.5 = f32[1,2,64,10,64]{2,0,4,3,1:T(1,128)S(1)} fusion(f32[8,2,64,10,64]{2,0,4,3,1:T(8,128)} %get-tuple-element.235, s32[]{:T(128)} %get-tuple-element.219), kind=kLoop, calls=%fused_computation.37.clone.1 | loop fusion | bytes 655364 | tf_op jit(solution)/shard_map/while/body/jit(dynamic_index_in_dim)/dynamic_slice | solution.py:118
  88.2 3.1 %constant_dynamic-slice_fusion.5 = f32[1,2,64,10,64]{2,0,4,3,1:T(1,128)S(1)} fusion(f32[8,2,64,10,64]{2,0,4,3,1:T(8,128)} %get-tuple-element.235, s32[]{:T(128)} %get-tuple-element.219), kind=kLoop, calls=%fused_computation.37.clone.1 | loop fusion | bytes 655364 | tf_op jit(solution)/shard_map/while/body/jit(dynamic_index_in_dim)/dynamic_slice | solution.py:118
  96.0 3.1 %constant_dynamic-slice_fusion.5 = f32[1,2,64,10,64]{2,0,4,3,1:T(1,128)S(1)} fusion(f32[8,2,64,10,64]{2,0,4,3,1:T(8,128)} %get-tuple-element.235, s32[]{:T(128)} %get-tuple-element.219), kind=kLoop, calls=%fused_computation.37.clone.1 | loop fusion | bytes 655364 | tf_op jit(solution)/shard_map/while/body/jit(dynamic_index_in_dim)/dynamic_slice | solution.py:118
  103.7 3.1 %constant_dynamic-slice_fusion.5 = f32[1,2,64,10,64]{2,0,4,3,1:T(1,128)S(1)} fusion(f32[8,2,64,10,64]{2,0,4,3,1:T(8,128)} %get-tuple-element.235, s32[]{:T(128)} %get-tuple-element.219), kind=kLoop, calls=%fused_computation.37.clone.1 | loop fusion | bytes 655364 | tf_op jit(solution)/shard_map/while/body/jit(dynamic_index_in_dim)/dynamic_slice | solution.py:118
  106.8 2.2 fusion.141
  111.5 3.1 %constant_dynamic-slice_fusion.5 = f32[1,2,64,10,64]{2,0,4,3,1:T(1,128)S(1)} fusion(f32[8,2,64,10,64]{2,0,4,3,1:T(8,128)} %get-tuple-element.235, s32[]{:T(128)} %get-tuple-element.219), kind=kLoop, calls=%fused_computation.37.clone.1 | loop fusion | bytes 655364 | tf_op jit(solution)/shard_map/while/body/jit(dynamic_index_in_dim)/dynamic_slice | solution.py:118
  114.6 2.2 fusion.141
  119.3 3.1 %constant_dynamic-slice_fusion.5 = f32[1,2,64,10,64]{2,0,4,3,1:T(1,128)S(1)} fusion(f32[8,2,64,10,64]{2,0,4,3,1:T(8,128)} %get-tuple-element.235, s32[]{:T(128)} %get-tuple-element.219), kind=kLoop, calls=%fused_computation.37.clone.1 | loop fusion | bytes 655364 | tf_op jit(solution)/shard_map/while/body/jit(dynamic_index_in_dim)/dynamic_slice | solution.py:118
  127.0 3.1 %constant_dynamic-slice_fusion.5 = f32[1,2,64,10,64]{2,0,4,3,1:T(1,128)S(1)} fusion(f32[8,2,64,10,64]{2,0,4,3,1:T(8,128)} %get-tuple-element.235, s32[]{:T(128)} %get-tuple-element.219), kind=kLoop, calls=%fused_computation.37.clone.1 | loop fusion | bytes 655364 | tf_op jit(solution)/shard_map/while/body/jit(dynamic_index_in_dim)/dynamic_slice | solution.py:118
  134.2 2.3 reduce-window.6
  138.9 7.7 %all-gather.2 = f32[8,1,10]{2,1,0:T(1,128)S(1)} all-gather(f32[2,1,10]{2,1,0:T(1,128)S(1)} %get-tuple-element.140), channel_id=4, replica_groups=mesh['seq_0'=4,'seq_1'=4,'seq_2'=2,'tp'=8] {'seq_1'}, dimensions={0}, use_global_device_ids=true | all-gather | bytes 400 | tf_op jit(solution)/shard_map/all_gather | solution.py:35
  148.2 2.3 bitcast_add_fusion.4
  150.8 37.7 %all-gather.7.cloned.1.call-done = f32[4,2,10,64,128]{4,3,2,1,0:T(8,128)} async-done(((f32[1,2,10,64,128]{4,3,2,1,0:T(8,128)}), f32[4,2,10,64,128]{4,3,2,1,0:T(8,128)}) %all-gather.7.cloned.1.call-update) | async-done | bytes 2621456 | tf_op jit(solution)/shard_map/all_gather | solution.py:35
  188.5 2.8 %multiply_add_fusion.1 = f32[1,2,10,64,128]{4,3,2,1,0:T(8,128)} fusion(f32[4,2,10,64,128]{4,3,2,1,0:T(8,128)} %all-gather.7.cloned.1.call-done, f32[2,10]{1,0:T(2,128)S(1)} %get-tuple-element.144, f32[2,10]{1,0:T(2,128)S(1)} %bitcast.251, f32[2,10]{1,0:T(2,128)S(1)} %bitcast.248, f32[2,10]{1,0:T(2,128)S(1)} %bitcast.254), kind=kLoop, calls=%fused_computation.98 | loop fusion | flops 1146880 | bytes 3277120 | tf_op jit(solution)/shard_map/add | solution.py:77
  191.8 7.1 %fusion.36 = f32[1024,640]{1,0:T(8,128)S(1)} fusion(bf16[1024,2560]{1,0:T(8,128)(2,1)} %bitcast.230, bf16[2560,640]{1,0:T(8,128)(2,1)} %param.13), kind=kOutput, calls=%fused_computation.56 | convolution fusion | flops 3356753920 | bytes 11141120 | tf_op jit(solution)/shard_map/dot_general | solution.py:96
  199.0 2.3 copy.110
  201.3 4.8 %reshape.160 = f32[2,512,10,64]{1,0,3,2:T(2,128)} reshape(f32[1024,640]{0,1:T(8,128)} %copy.110) | data formatting | bytes 5242880 | tf_op jit(solution)/shard_map/convert_element_type | solution.py:143
  206.1 8.6 %all_gather.32 = f32[4,2,10]{2,1,0:T(2,128)S(1)} all-gather(f32[1,2,10]{2,1,0:T(2,128)S(1)} %bitcast.259), channel_id=1, replica_groups=mesh['seq_0'=4,'seq_1'=4,'seq_2'=2,'tp'=8] {'seq_0'}, dimensions={0}, use_global_device_ids=true | all-gather | bytes 400 | tf_op jit(solution)/shard_map/all_gather | solution.py:35
  214.6 9.2 %copy.102 = f32[2,8,64,10,64]{2,1,4,3,0:T(8,128)} copy(f32[2,8,64,10,64]{2,4,3,0,1:T(8,128)} %bitcast.237) | data formatting | bytes 5242880 | tf_op jit(solution)/shard_map/transpose | solution.py:129
  223.8 5.2 %reshape.155 = f32[2,512,10,64]{1,3,2,0:T(8,128)} reshape(f32[2,8,64,10,64]{2,1,4,3,0:T(8,128)} %copy.102) | data formatting | bytes 5242880 | tf_op jit(solution)/shard_map/reshape | solution.py:129
  229.3 9.1 %multiply_reduce_fusion = (f32[2,512]{1,0:T(2,128)S(1)}, f32[2,512,10,64]{1,3,2,0:T(8,128)}) fusion(f32[2,512,10,64]{1,0,3,2:T(2,128)S(1)} %copy-done.6, f32[2,512,10,64]{1,3,2,0:T(8,128)} %reshape.155, f32[2,512,10]{1,2,0:T(8,128)S(1)} %copy.108, f32[4,2,10,64,128]{4,3,2,1,0:T(8,128)} %all-gather.9.cloned.1.call-done, ...), kind=kOutput, calls=%fused_computation.51 | convolution fusion | flops 1017609216 | bytes 14988234 | tf_op jit(solution)/shard_map/btn,bhpn->bthp/dot_general | solution.py:139
  238.4 3.2 %copy.109 = f32[2,512,640]{2,1,0:T(8,128)} copy(f32[2,512,640]{1,2,0:T(8,128)} %bitcast.238) | data formatting | bytes 5242880 | tf_op jit(solution)/shard_map/reshape | solution.py:141
  241.6 13.7 %psum.7 = f32[2,512,1]{1,0,2:T(2,128)S(1)} all-reduce(f32[2,512,1]{1,0,2:T(2,128)S(1)} %bitcast.261), channel_id=1, replica_groups=mesh['seq_0'=4,'seq_1'=4,'seq_2'=2,'tp'=8] {'tp'}, use_global_device_ids=true, to_apply=%region_6.7 | all-reduce | flops 1024 | bytes 8192 | tf_op jit(solution)/shard_map/psum | solution.py:146
  255.4 4.6 %multiply_convert_fusion = bf16[2,512,640]{2,1,0:T(8,128)(2,1)} fusion(f32[2,512,640]{2,1,0:T(8,128)} %copy.109, f32[2,512,640]{2,1,0:T(8,128)} %bitcast.233, f32[640]{0:T(1024)S(1)} %copy-done.12, f32[2,512]{1,0:T(2,128)S(1)} %rsqrt_bitcast_fusion), kind=kLoop, calls=%fused_computation.50 | loop fusion | flops 5242880 | bytes 6560256 | tf_op jit(solution)/shard_map/convert_element_type | solution.py:147
  (203 shorter events, 50.7 us)
Async XLA Ops:
  6.5 1.9 copy-start
  6.5 141.7 %all-gather.11.cloned.1.call-start = ((), (), s32[]{:S(2)}) async-start(), calls=%async_computation.2 | async-start | bytes 1966080 | tf_op jit(solution)/shard_map/all_gather | solution.py:35
  8.5 6.2 %copy-start.3 = (bf16[2,512,2560]{2,1,0:T(8,128)(2,1)S(1)}, bf16[2,512,2560]{2,1,0:T(8,128)(2,1)}, u32[]{:S(2)}) copy-start(bf16[2,512,2560]{2,1,0:T(8,128)(2,1)} %param.12) | copy-start | bytes 15728644
  8.5 6.2 %copy-start.9 = (bf16[2560,32]{0,1:T(8,128)(2,1)S(1)}, bf16[2560,32]{0,1:T(8,128)(2,1)}, u32[]{:S(2)}) copy-start(bf16[2560,32]{0,1:T(8,128)(2,1)} %param.15) | copy-start | bytes 491524
  40.1 14.6 %copy-start.11 = (f32[4,640]{1,0:T(4,128)S(1)}, f32[4,640]{1,0:T(4,128)}, u32[]{:S(2)}) copy-start(f32[4,640]{1,0:T(4,128)} %param.17) | copy-start | bytes 30724
  40.1 14.6 %copy-start.15 = (f32[10]{0:T(128)S(1)}, f32[10]{0:T(128)}, u32[]{:S(2)}) copy-start(f32[10]{0:T(128)} %param.20) | copy-start | bytes 124
  40.1 14.6 %copy-start.10 = (bf16[2560,10]{0,1:T(8,128)(2,1)S(1)}, bf16[2560,10]{0,1:T(8,128)(2,1)}, u32[]{:S(2)}) copy-start(bf16[2560,10]{0,1:T(8,128)(2,1)} %param.16) | copy-start | bytes 153604
  40.1 14.6 %copy-start.14 = (f32[10]{0:T(128)S(1)}, f32[10]{0:T(128)}, u32[]{:S(2)}) copy-start(f32[10]{0:T(128)} %param.19) | copy-start | bytes 124
  44.6 14.2 %copy-start.13 = (f32[4,256]{1,0:T(4,128)S(1)}, f32[4,256]{1,0:T(4,128)}, u32[]{:S(2)}) copy-start(f32[4,256]{1,0:T(4,128)} %param.18) | copy-start | bytes 12292
  44.6 14.6 %collective-permute-start = (bf16[2,3,896]{2,1,0:T(4,128)(2,1)S(1)}, bf16[2,3,896]{2,1,0:T(4,128)(2,1)S(1)}, u32[]{:S(2)}, u32[]{:S(2)}) collective-permute-start(bf16[2,3,896]{2,1,0:T(4,128)(2,1)S(1)} %slice.155), channel_id=1, source_target_pairs={{0,8},{8,16},{16,24},{24,32},{32,40},{40,48},{48,56},{56,64},{64,7... | collective-permute-start | bytes 32264 | tf_op jit(solution)/shard_map/ppermute | solution.py:21
  61.7 2.2 copy-start.4
  66.2 4.9 %copy-start.7 = (f32[2,512,128]{2,1,0:T(8,128)S(1)}, f32[2,512,128]{2,1,0:T(8,128)}, u32[]{:S(2)}) copy-start(f32[2,512,128]{2,1,0:T(8,128)} %get-tuple-element.127) | copy-start | bytes 1572868
  66.2 4.9 %copy-start.8 = (f32[2,512,128]{2,1,0:T(8,128)S(1)}, f32[2,512,128]{2,1,0:T(8,128)}, u32[]{:S(2)}) copy-start(f32[2,512,128]{2,1,0:T(8,128)} %get-tuple-element.128) | copy-start | bytes 1572868
  133.3 0.8 copy-start.2
  134.1 54.4 %all-gather.7.cloned.1.call-start = ((), (), s32[]{:S(2)}) async-start(), calls=%async_computation | async-start | bytes 3276800 | tf_op jit(solution)/shard_map/all_gather | solution.py:35
  150.5 78.8 %all-gather.9.cloned.1.call-start = ((), (), s32[]{:S(2)}) async-start(), calls=%async_computation.1 | async-start | bytes 3276800 | tf_op jit(solution)/shard_map/all_gather | solution.py:35
  199.0 7.1 %copy-start.5 = (f32[1024,640]{1,0:T(8,128)}, f32[1024,640]{1,0:T(8,128)S(1)}, u32[]{:S(2)}) copy-start(f32[1024,640]{1,0:T(8,128)S(1)} %fusion.36) | copy-start | bytes 7864324
  223.8 5.5 %copy-start.6 = (f32[2,512,10,64]{1,0,3,2:T(2,128)S(1)}, f32[2,512,10,64]{1,0,3,2:T(2,128)}, u32[]{:S(2)}) copy-start(f32[2,512,10,64]{1,0,3,2:T(2,128)} %reshape.160) | copy-start | bytes 7864324
  238.4 17.0 %copy-start.12 = (f32[640]{0:T(1024)S(1)}, f32[640]{0:T(1024)}, u32[]{:S(2)}) copy-start(f32[640]{0:T(1024)} %param.21) | copy-start | bytes 7684
  255.3 4.7 %copy-start.1 = (bf16[2560,640]{1,0:T(8,128)(2,1)S(1)}, bf16[2560,640]{1,0:T(8,128)(2,1)}, u32[]{:S(2)}) copy-start(bf16[2560,640]{1,0:T(8,128)(2,1)} %param.14) | copy-start | bytes 9830404
Sparse Core Ops, SparseCore 0:
  134.3 13.8 all-gather.10
  150.6 37.8 all-gather.6
  191.4 37.7 all-gather.8
where the time goes:
time: 271 us; the launch traced here: 267 us
  local copies, waits for them, and re-layouts  69.9 us (26%)
  matrix products  59.8 us (22%)
  blocking collectives  55.5 us (20%)
  waiting for transfers between devices  39.6 us (15%)
  other arithmetic  17.2 us (6%)
  between operations  13.4 us (5%)
  starting transfers between devices  10.4 us (4%)
    all_gather x3, waiting for transfers between devices, entering(): pieces = jax.tree.map(lambda part: lax.all_gather(part, axis), so_far)  39.6 us
    dynamic_slice x32, local copies, waits for them, and re-layouts, on_device(): lax.scan(block_step, initial, (to_blocks(values, batch_size, blocks), to_...  26.5 us
    all_gather x1, blocking collectives, on_device(): bc_pre = lax.all_gather(bc_part, 'tp', axis=1, tiled=True)  23.7 us
    all_gather x3, blocking collectives, entering(): pieces = jax.tree.map(lambda part: lax.all_gather(part, axis), so_far)  18.1 us
    dot_general x8, matrix products, block_step(): jnp.einsum('bijh,bjhp->bihp', mixing, values, precision=lax.Precision.HIG...  17.6 us
    psum x1, blocking collectives, on_device(): whole_sq = lax.psum(squares, 'tp')  13.7 us
    ppermute x1, starting transfers between devices, passed_along(): return lax.ppermute(block, axis, route)  10.1 us
    transpose x1, local copies, waits for them, and re-layouts, on_device(): jnp.moveaxis(outputs, 0, 1)  9.16 us
  transfers between devices with their start and end apart: 4, of which 3 were waited for; matrix products, arithmetic and copies ran while one was open for 14% of the time, Pallas kernels for 0%

commit v1 on v0

v1 whole, which is shorter than its diff:
```python
import jax
import jax.numpy as jnp
from jax import lax
from jax.experimental import pallas as pl
from jax.experimental.pallas import tpu as pltpu
from jax.sharding import PartitionSpec as P

MESH = pl.DeviceIdType.MESH
F32, BF16 = jnp.float32, jnp.bfloat16

NS, NZ = 32, 8
D, DI = 2560, 5120
CI = 640
LEN = 512
Q = 128
NB = LEN // Q
PAD = 16
HL = 32
HEADS = 10
EPS = 1e-05


def dot(a, b):
    return jnp.dot(a, b, preferred_element_type=F32)


def silu(x):
    half = 0.5 * x
    return half + half * jnp.tanh(half)


def split(x):
    high = x.astype(BF16)
    low = (x - high.astype(F32)).astype(BF16)
    return jnp.concatenate([high, low], axis=1)


def kernel(
    hid, gw, vw, bw, sw, vconv, bconv, sbias, lrate, gain, out,
    hx, w, bwv, swv, cv, bcv, sb, lr, gn, prm, tap, ee, bs, vp, bct, cmat, bmat,
    av, ev, fg, g, rx, dsum, dall, dxl, dx, vv, sbl, st, p1, po, pin, ssm, ssa, osc,
    ld, lo, hs, hr, bsend, brecv, bhs, bhr, dsend, drecv, s1, r1, s2, r2, zs, zr,
):
    me, z = lax.axis_index("seq"), lax.axis_index("tp")
    core, chip = lax.rem(me, 2), lax.div(me, 2)

    def remote(src, dst, ss, rs, seq=None, tp=None):
        where = {"seq": me if seq is None else seq, "tp": z if tp is None else tp}
        return pltpu.make_async_remote_copy(
            src_ref=src, dst_ref=dst, send_sem=ss, recv_sem=rs, device_id=where, device_id_type=MESH
        )

    small = [
        pltpu.make_async_copy(src, dst, ld.at[9 + n])
        for n, (src, dst) in enumerate(
            [(vconv, cv), (bconv, bcv), (sbias, sb), (lrate, lr), (gain, gn)]
        )
    ]
    load_b = pltpu.make_async_copy(bw, bwv, ld.at[0])
    load_s = pltpu.make_async_copy(sw, swv, ld.at[1])
    load_v0 = pltpu.make_async_copy(vw.at[:, 0:128], w.at[:, 128:256], ld.at[2])
    load_v1 = pltpu.make_async_copy(vw.at[:, 128:CI], w.at[:, 256:768], ld.at[7])
    load_g = pltpu.make_async_copy(gw, w.at[:, 768:1408], ld.at[8])

    def load_h(i):
        s, h = i // 2, i % 2
        return pltpu.make_async_copy(
            hid.at[s, pl.ds(256 * h, 256)], hx.at[s, pl.ds(PAD + 256 * h, 256)], ld.at[3 + i]
        )

    for copy in small:
        copy.start()
    load_b.start()
    load_s.start()
    load_v0.start()
    for i in range(4):
        load_h(i).start()
    load_g.start()
    load_v1.start()

    barrier = pltpu.get_barrier_semaphore()

    def greet_seq(r, _):
        pl.semaphore_signal(
            barrier, inc=1, device_id={"seq": lax.rem(me + r, NS), "tp": z}, device_id_type=MESH
        )
        return 0

    def greet_tp(r, _):
        pl.semaphore_signal(
            barrier, inc=1, device_id={"seq": me, "tp": lax.rem(z + r, NZ)}, device_id_type=MESH
        )
        return 0

    lax.fori_loop(1, NS, greet_seq, 0)
    lax.fori_loop(1, NZ, greet_tp, 0)

    row = lax.broadcasted_iota(jnp.int32, (256, CI), 0)
    col = lax.broadcasted_iota(jnp.int32, (256, CI), 1)
    ee[...] = jnp.where((row & 127) == HL + (col >> 6), 1.0, 0.0).astype(BF16)
    tri_at = lax.broadcasted_iota(jnp.int32, (Q, Q), 0) >= lax.broadcasted_iota(
        jnp.int32, (Q, Q), 1
    )
    tri = jnp.where(tri_at, 1.0, 0.0).astype(BF16)
    prm[...] = jnp.zeros((8, 128), F32)
    dsum[...] = jnp.zeros((8, 128), F32)
    w[:, 0:128] = jnp.zeros((D, 128), BF16)
    for s in range(2):
        hx[s, 0:8, :] = jnp.zeros((8, D), BF16)

    @pl.when(me == 0)
    def _():
        for s in range(2):
            hx[s, 8:16, :] = jnp.zeros((8, D), BF16)

    for copy in small:
        copy.wait()
    prm[0:1, HL : HL + HEADS] = sb[...]
    prm[1:2, HL : HL + HEADS] = lr[...]
    for k in range(4):
        for h in range(2):
            taps = bcv[k : k + 1, 128 * h : 128 * h + 128]
            tap[2 * k + h] = jnp.broadcast_to(taps, (128, 128)).T
    load_b.wait()
    w[:, 0:HL] = bwv[...]
    load_s.wait()
    w[:, HL : HL + HEADS] = swv[...]
    load_v0.wait()

    def first(i, _):
        s, h = lax.div(i, 2), lax.rem(i, 2)
        at = pl.multiple_of(256 * h, 256)
        pltpu.make_async_copy(
            hid.at[s, pl.ds(at, 256)], hx.at[s, pl.ds(PAD + at, 256)], ld.at[3 + i]
        ).wait()
        got = dot(hx[s, pl.ds(PAD + at, 256), :], w[:, 0:256])
        bs[s, pl.ds(at, 256), :] = got[:, 0:128]
        vp[s, pl.ds(PAD + at, 256), 0:128] = got[:, 128:256]
        return 0

    lax.fori_loop(0, 4, first, 0)

    def turn(s, _):
        for b in range(NB):
            got = bs[s, Q * b : Q * b + Q, :].T
            bct[s, z, :, 128 + Q * b : 128 + Q * b + Q] = got[0:32, :].astype(BF16)
        return 0

    lax.fori_loop(0, 2, turn, 0)

    pl.semaphore_wait(barrier, NS - 1 + NZ - 1)

    def bulk(s, owner, peer):
        part = bct.at[s, owner, :, 128:640]
        return remote(part, part, bsend.at[s, peer], brecv.at[s, owner], tp=peer)

    def send_bulk(n, _):
        s, r = lax.div(n, NZ - 1), 1 + lax.rem(n, NZ - 1)
        bulk(s, z, lax.rem(z + r, NZ)).start()
        return 0

    lax.fori_loop(0, 2 * (NZ - 1), send_bulk, 0)

    def halo():
        return remote(hx.at[:, 520:528], hx.at[:, 8:16], hs, hr, seq=lax.rem(me + 1, NS))

    @pl.when(me < NS - 1)
    def _():
        halo().start()

    lane = lax.broadcasted_iota(jnp.int32, (Q, 128), 1)
    is_head = (lane >= HL) & (lane < HL + HEADS)
    rate = jnp.exp(prm[1:2, :])

    def steps(s, _):
        so_far = jnp.zeros((1, 128), F32)
        halves, ahead = [], []
        for b in range(NB):
            x = bs[s, Q * b : Q * b + Q, :] + prm[0:1, :]
            size = jnp.maximum(x, 0.0) + jnp.log1p(jnp.exp(-jnp.abs(x)))
            size = jnp.where(is_head, size, 0.0)
            sums = dot(tri, split(-size * rate))
            cum = sums[:, 0:128] + sums[:, 128:256]
            total = cum[Q - 1 : Q, :]
            mid = 0.5 * total
            av[s, Q * b : Q * b + Q, :] = dot(split(size * jnp.exp(mid - cum)), ee[...])
            ev[s, Q * b : Q * b + Q, :] = dot(split(jnp.exp(cum - mid)), ee[...])
            halves.append(jnp.exp(mid))
            ahead.append(jnp.exp(so_far + mid))
            so_far = so_far + total
        rows = jnp.concatenate(halves + ahead + [jnp.zeros((8, 128), F32)], axis=0)
        rx[s] = dot(split(rows), ee[...])[0:8, :]
        dsum[pl.ds(s, 1), :] = so_far
        return 0

    lax.fori_loop(0, 2, steps, 0)

    def decay(owner, peer):
        src = dsum if owner is None else dall.at[owner]
        slot = me if owner is None else owner
        return remote(src, dall.at[slot], dsend.at[peer], drecv.at[slot], seq=peer)

    def send_decay(r, _):
        decay(None, lax.rem(me + r, NS)).start()
        return 0

    lax.fori_loop(1, NS, send_decay, 0)
    dall[me] = dsum[...]

    load_g.wait()

    def gate(s, _):
        for at, wide in ((0, 256), (256, 256), (512, 128)):
            got = dot(hx[s, PAD : PAD + LEN, :], w[:, 768 + at : 768 + at + wide])
            fg[s, :, at : at + wide] = silu(got) * ev[s, :, at : at + wide]
        return 0

    lax.fori_loop(0, 2, gate, 0)

    @pl.when(me > 0)
    def _():
        halo().wait_recv()

    both = jnp.concatenate([hx[0, 8:16, :], hx[1, 8:16, :]], axis=0)
    got = dot(both, w[:, 0:256])
    for s in range(2):
        rows = got[8 * s : 8 * s + 8, :]
        vp[s, 8:16, 0:128] = rows[:, 128:256]
        tail = jnp.concatenate([jnp.zeros((120, 128), F32), rows[:, 0:128]], axis=0).T
        bct[s, z, :, 0:128] = tail[0:32, :].astype(BF16)

    def bc_halo(owner, peer):
        part = bct.at[:, owner, :, 0:128]
        return remote(part, part, bhs.at[peer], bhr.at[owner], tp=peer)

    def send_bc_halo(r, _):
        bc_halo(z, lax.rem(z + r, NZ)).start()
        return 0

    lax.fori_loop(1, NZ, send_bc_halo, 0)

    load_v1.wait()

    def value(s, _):
        for at in (0, 256):
            vp[s, :, 128 + at : 384 + at] = dot(hx[s], w[:, 256 + at : 512 + at])
        for b in range(NB):
            for c in range(5):
                lanes = slice(128 * c, 128 * c + 128)
                rows = vp[s, 8 + Q * b : 8 + Q * b + Q + 8, lanes]
                mixed = cv[0:1, lanes] * rows[5 : 5 + Q]
                for k in range(1, 4):
                    mixed = mixed + cv[k : k + 1, lanes] * rows[5 + k : 5 + k + Q]
                here = (s, slice(Q * b, Q * b + Q), lanes)
                vv[here] = (silu(mixed) * av[here]).astype(BF16)
        return 0

    lax.fori_loop(0, 2, value, 0)

    def wait_bc_halo(r, _):
        peer = lax.rem(z + r, NZ)
        bc_halo(peer, peer).wait_recv()
        return 0

    lax.fori_loop(1, NZ, wait_bc_halo, 0)

    def first_hop(source, k, s):
        owner = 2 * k + s
        return remote(st.at[s, k], p1.at[source], s1.at[owner], r1.at[source], seq=owner)

    def states(s, _):
        def wait_bulk(r, _):
            peer = lax.rem(z + r, NZ)
            bulk(s, peer, peer).wait_recv()
            return 0

        lax.fori_loop(1, NZ, wait_bulk, 0)
        for h in range(2):
            x = bct[s, 4 * h : 4 * h + 4].astype(F32).reshape(128, 640)
            turned = [pltpu.roll(x, 3 - k, 1) for k in range(3)] + [x]
            for b in range(NB):
                lanes = slice(128 + Q * b, 256 + Q * b)
                mixed = tap[h] * turned[0][:, lanes]
                for k in range(1, 4):
                    mixed = mixed + tap[2 * k + h] * turned[k][:, lanes]
                mixed = silu(mixed)
                if h == 0:
                    bmat[s, :, Q * b : Q * b + Q] = mixed.astype(BF16)
                else:
                    cmat[s, Q * b : Q * b + Q, :] = mixed.T.astype(BF16)
        state = None
        for b in range(NB):
            half = rx[s, b : b + 1, :]
            added = dot(bmat[s, :, Q * b : Q * b + Q], vv[s, Q * b : Q * b + Q, :]) * half
            if state is None:
                sbl[s, b] = jnp.zeros((128, CI), BF16)
                state = added
            else:
                lifted = state * half
                sbl[s, b] = lifted.astype(BF16)
                state = lifted * half + added
        for k in range(16):
            st[s, k] = state[8 * k : 8 * k + 8, :].astype(BF16)

        def send(r, _):
            k = lax.rem(chip + r, 16)

            @pl.when(2 * k + s != me)
            def _():
                first_hop(me, k, s).start()

            return 0

        lax.fori_loop(0, 16, send, 0)
        return 0

    lax.fori_loop(0, 2, states, 0)
    p1[me] = st[core, chip]

    def within(s, _):
        for b in range(NB):
            rows = slice(Q * b, Q * b + Q)
            c_rows = cmat[s, rows, :]
            scores = dot(c_rows, bmat[s, :, rows])
            scores = jnp.where(tri_at, scores, 0.0).astype(BF16)
            left = jnp.concatenate([scores, c_rows], axis=1)
            right = jnp.concatenate([vv[s, rows, :], sbl[s, b]], axis=0)
            g[s, rows, :] = dot(left, right)
        return 0

    lax.fori_loop(0, 2, within, 0)

    def wait_decay(r, _):
        source = lax.rem(me + r, NS)
        decay(source, source).wait_recv()
        return 0

    lax.fori_loop(1, NS, wait_decay, 0)

    def pick(j, _):
        dxl[pl.ds(j, 1), :] = dall[j, pl.ds(core, 1), :]
        return 0

    lax.fori_loop(0, NS, pick, 0)
    dx[...] = dot(split(jnp.exp(dxl[...])), ee[...])

    def wait_first(r, _):
        source = lax.rem(me + r, NS)
        first_hop(source, chip, core).wait_recv()
        return 0

    lax.fori_loop(1, NS, wait_first, 0)

    def scan(j, so_far):
        po[j] = so_far.astype(BF16)
        return so_far * dx[pl.ds(j, 1), :] + p1[j].astype(F32)

    lax.fori_loop(0, NS, scan, jnp.zeros((8, CI), F32))

    def second_hop(target, source):
        slot = pin.at[lax.rem(source, 2), lax.div(source, 2)]
        return remote(po.at[target], slot, s2.at[target], r2.at[source], seq=target)

    def send_second(r, _):
        second_hop(lax.rem(me + r, NS), me).start()
        return 0

    lax.fori_loop(1, NS, send_second, 0)
    pin[core, chip] = po[me]

    ones = jnp.ones((16, CI), BF16)
    at_row = lax.broadcasted_iota(jnp.int32, (8, 128), 0)

    def finish(s, squares):
        def wait_second(k, _):
            source = 2 * k + s

            @pl.when(source != me)
            def _():
                second_hop(source, source).wait_recv()

            return 0

        lax.fori_loop(0, 16, wait_second, 0)
        arrived = pin[s].astype(F32).reshape(128, CI)
        for b in range(NB):
            rows = slice(Q * b, Q * b + Q)
            scaled = (arrived * rx[s, 4 + b : 5 + b, :]).astype(BF16)
            gated = fg[s, rows, :] * (g[s, rows, :] + dot(cmat[s, rows, :], scaled))
            g[s, rows, :] = gated
            sq = (gated * gated).astype(BF16)
            summed = lax.dot_general(
                ones, sq, (((1,), (1,)), ((), ())), preferred_element_type=F32
            )[0:8, :]
            squares = jnp.where(at_row == 4 * s + b, summed, squares)
        return squares

    ssm[...] = lax.fori_loop(0, 2, finish, jnp.zeros((8, 128), F32))

    def total_sq(owner, peer):
        return remote(ssm, ssa.at[owner], zs.at[peer], zr.at[owner], tp=peer)

    def send_sq(r, _):
        total_sq(z, lax.rem(z + r, NZ)).start()
        return 0

    lax.fori_loop(1, NZ, send_sq, 0)
    ssa[z] = ssm[...]

    def wait_sq(r, _):
        peer = lax.rem(z + r, NZ)
        total_sq(peer, peer).wait_recv()
        return 0

    lax.fori_loop(1, NZ, wait_sq, 0)
    scale = lax.rsqrt(jnp.sum(ssa[...], axis=0) * (1.0 / DI) + EPS)
    for s in range(2):
        for b in range(NB):
            rows = slice(Q * b, Q * b + Q)
            by_token = jnp.broadcast_to(scale[4 * s + b : 4 * s + b + 1, :], (128, 128)).T
            for c in range(5):
                lanes = slice(128 * c, 128 * c + 128)
                osc[s, rows, lanes] = (g[s, rows, lanes] * by_token * gn[:, lanes]).astype(BF16)
        pltpu.make_async_copy(osc.at[s], out.at[s], lo.at[s]).start()

    def sent_tp(r, _):
        peer = lax.rem(z + r, NZ)
        bulk(0, z, peer).wait_send()
        bulk(1, z, peer).wait_send()
        bc_halo(z, peer).wait_send()
        total_sq(z, peer).wait_send()
        return 0

    lax.fori_loop(1, NZ, sent_tp, 0)

    def sent_seq(r, _):
        peer = lax.rem(me + r, NS)
        decay(None, peer).wait_send()
        first_hop(me, lax.div(peer, 2), lax.rem(peer, 2)).wait_send()
        second_hop(peer, me).wait_send()
        return 0

    lax.fori_loop(1, NS, sent_seq, 0)

    @pl.when(me < NS - 1)
    def _():
        halo().wait_send()

    for s in range(2):
        pltpu.make_async_copy(osc.at[s], out.at[s], lo.at[s]).wait()


def on_device(hid, gw, vw, bw, sw, vconv, bconv, sbias, lrate, gain):
    dma = pltpu.SemaphoreType.DMA
    vmem = pltpu.VMEM
    any_space = pl.BlockSpec(memory_space=pl.ANY)
    scratch = [
        vmem((2, PAD + LEN, D), BF16),
        vmem((D, 1408), BF16),
        vmem((D, 32), BF16),
        vmem((D, HEADS), BF16),
        vmem((4, CI), F32),
        vmem((4, 256), F32),
        vmem((1, HEADS), F32),
        vmem((1, HEADS), F32),
        vmem((1, CI), F32),
        vmem((8, 128), F32),
        vmem((8, 128, 128), F32),
        vmem((256, CI), BF16),
        vmem((2, LEN, 128), F32),
        vmem((2, PAD + LEN, CI), F32),
        vmem((2, NZ, 32, 128 + LEN), BF16),
        vmem((2, LEN, 128), BF16),
        vmem((2, 128, LEN), BF16),
        vmem((2, LEN, CI), F32),
        vmem((2, LEN, CI), F32),
        vmem((2, LEN, CI), F32),
        vmem((2, LEN, CI), F32),
        vmem((2, 8, CI), F32),
        vmem((8, 128), F32),
        vmem((NS, 8, 128), F32),
        vmem((NS, 128), F32),
        vmem((NS, CI), F32),
        vmem((2, LEN, CI), BF16),
        vmem((2, NB, 128, CI), BF16),
        vmem((2, 16, 8, CI), BF16),
        vmem((NS, 8, CI), BF16),
        vmem((NS, 8, CI), BF16),
        vmem((2, 16, 8, CI), BF16),
        vmem((8, 128), F32),
        vmem((NZ, 8, 128), F32),
        vmem((2, LEN, CI), BF16),
        dma((14,)),
        dma((2,)),
        dma,
        dma,
        dma((2, NZ)),
        dma((2, NZ)),
        dma((NZ,)),
        dma((NZ,)),
        dma((NS,)),
        dma((NS,)),
        dma((NS,)),
        dma((NS,)),
        dma((NS,)),
        dma((NS,)),
        dma((NZ,)),
        dma((NZ,)),
    ]
    return pl.pallas_call(
        kernel,
        out_shape=jax.ShapeDtypeStruct((2, LEN, CI), BF16),
        in_specs=[any_space] * 10,
        out_specs=any_space,
        scratch_shapes=scratch,
        compiler_params=pltpu.CompilerParams(
            collective_id=0, has_side_effects=True, vmem_limit_bytes=56 * 2**20
        ),
    )(
        hid, gw, vw, bw, sw, vconv, bconv,
        sbias.reshape(1, HEADS), lrate.reshape(1, HEADS), gain.reshape(1, CI),
    )


def solution(mesh):
    placed = (
        P(None, "seq", None),
        P(None, "tp"),
        P(None, "tp"),
        P(None, "tp"),
        P(None, "tp"),
        P(None, "tp"),
        P(),
        P("tp"),
        P("tp"),
        P("tp"),
    )
    return jax.shard_map(
        on_device, mesh=mesh, in_specs=placed, out_specs=P(None, "seq", "tp"), check_vma=False
    )
```

time: 271 us -> 59.3 us (0.22); the launches traced: 267 us -> 59.1 us
  local copies, waits for them, and re-layouts: 69.9 us -> 7.8 us
  matrix products: 59.8 us -> 0 us
  blocking collectives: 55.5 us -> 0 us
  Pallas kernels: 0 us -> 51.3 us
  waiting for transfers between devices: 39.6 us -> 0 us
  other arithmetic: 17.2 us -> 0 us
  between operations: 13.4 us -> 0.01 us
  starting transfers between devices: 10.4 us -> 0 us
    dot_general x37 -> x0, matrix products: 59.8 us -> none  [the longest x8 17.6 us: block_step(): jnp.einsum('bijh,bjhp->bihp', mixing, values, precision=lax.Precision.HIG...]
    pallas_call x0 -> x1, Pallas kernels: none -> 51.3 us  [on_device(): pl.pallas_call(kernel, out_shape=jax.ShapeDtypeStruct((2, LEN, CI), BF16)...]
    all_gather x4 -> x0, blocking collectives: 41.8 us -> none  [the longest x1 23.7 us: on_device(): bc_pre = lax.all_gather(bc_part, 'tp', axis=1, tiled=True)]
    all_gather x3 -> x0, waiting for transfers between devices: 39.6 us -> none  [entering(): pieces = jax.tree.map(lambda part: lax.all_gather(part, axis), so_far)]
    dynamic_slice x32 -> x0, local copies, waits for them, and re-layouts: 26.5 us -> none  [on_device(): lax.scan(block_step, initial, (to_blocks(values, batch_size, blocks), to_...]
    psum x1 -> x0, blocking collectives: 13.7 us -> none  [on_device(): whole_sq = lax.psum(squares, 'tp')]
    reshape x7 -> x1, local copies, waits for them, and re-layouts: 11.7 us -> 1.28 us  [on_device(): gain.reshape(1, CI)]
    ppermute x1 -> x0, starting transfers between devices: 10.1 us -> none  [passed_along(): return lax.ppermute(block, axis, route)]
  transfers between devices with their start and end apart: 4 -> 0, of which waited for: 3 -> 0; matrix products, arithmetic and copies ran while one was open for 14% -> 0% of each run, Pallas kernels for 0% -> 0%
where the time goes in v1:
time: 59.3 us; the launch traced here: 59.1 us
  Pallas kernels  51.3 us (87%)
  local copies, waits for them, and re-layouts  7.8 us (13%)
    pallas_call x1, Pallas kernels, on_device(): pl.pallas_call(kernel, out_shape=jax.ShapeDtypeStruct((2, LEN, CI), BF16)...  51.3 us
    unnamed x3, local copies, waits for them, and re-layouts  6.52 us
    reshape x1, local copies, waits for them, and re-layouts, on_device(): gain.reshape(1, CI)  1.28 us

profile of v1, /device:TPU:1, one launch (start us, length us, event | category | flops | bytes accessed | tf_op | source)
XLA Modules:
  0.0 59.1 jit_solution(6551467561725214523)
XLA Ops:
  0.0 1.3 %reshape.11.gain = f32[1,640]{1,0:T(1,128)} reshape(f32[640]{0:T(1024)} %param.19) | data formatting | bytes 5120 | tf_op jit(solution)/shard_map/reshape | solution.py:521
  1.3 2.0 %copy.11.bw = bf16[2560,32]{1,0:T(8,128)(2,1)} copy(bf16[2560,32]{0,1:T(8,128)(2,1)} %param.13) | data formatting | bytes 327680 | tf_op args[3]
  3.3 2.0 %copy.12.sw = bf16[2560,10]{1,0:T(8,128)(2,1)} copy(bf16[2560,10]{0,1:T(8,128)(2,1)} %param.14) | data formatting | bytes 102400 | tf_op args[4]
  5.3 51.3 %shard_map.100 = bf16[2,512,640]{2,1,0:T(8,128)(2,1)} custom-call(bf16[2,512,2560]{2,1,0:T(8,128)(2,1)} %hid.1, bf16[2560,640]{1,0:T(8,128)(2,1)} %gw.1, bf16[2560,640]{1,0:T(8,128)(2,1)} %vw.1, bf16[2560,32]{1,0:T(8,128)(2,1)} %copy.11.bw, bf16[2560,10]{1,0:T(8,128)(2,1)} %copy.12.sw, f32[4,640]{1,0:T(4,128)} %vconv.1, f32[4,256]{1,0:T(4,128)} %bconv.1, ...), custom_call_target="tpu_custom_call" | custom-call | tf_op jit(solution)/shard_map/pallas_call | solution.py:510
  56.6 2.5 %copy.14 = bf16[2,512,640]{2,1,0:T(8,128)(2,1)} copy(bf16[2,512,640]{2,1,0:T(8,128)(2,1)} %shard_map.100) | data formatting | bytes 2621440

commit v2 on v1

v2 whole, which is shorter than its diff:
```python
import jax
import jax.numpy as jnp
from jax import lax
from jax.experimental import pallas as pl
from jax.experimental.pallas import tpu as pltpu
from jax.sharding import PartitionSpec as P

MESH = pl.DeviceIdType.MESH
F32, BF16 = jnp.float32, jnp.bfloat16

NS, NZ = 32, 8
D, DI = 2560, 5120
CI = 640
LEN = 512
Q = 128
NB = LEN // Q
PAD = 16
HL = 32
HEADS = 10
EPS = 1e-05


def dot(a, b):
    return jnp.dot(a, b, preferred_element_type=F32)


def silu(x):
    half = 0.5 * x
    return half + half * jnp.tanh(half)


def split(x):
    high = x.astype(BF16)
    low = (x - high.astype(F32)).astype(BF16)
    return jnp.concatenate([high, low], axis=1)


def kernel(
    hid, gw, vw, bw, sw, vconv, bconv, sbias, lrate, gain, out,
    hx, w, bwv, swv, cv, bcv, sb, lr, gn, prm, tap, ee, bs, vp, bct, cmat, bmat,
    av, ev, fg, g, rx, dsum, dall, dxl, dx, bhl, vv, sbl, st, p1, po, pin, ssm, ssa, osc,
    ld, lo, hs, hr, bsend, brecv, dsend, drecv, s1, r1, s2, r2, zs, zr,
):
    me, z = lax.axis_index("seq"), lax.axis_index("tp")
    core, chip = me & 1, lax.div(me, 2)

    def remote(src, dst, ss, rs, seq=None, tp=None):
        where = {"seq": me if seq is None else seq, "tp": z if tp is None else tp}
        return pltpu.make_async_remote_copy(
            src_ref=src, dst_ref=dst, send_sem=ss, recv_sem=rs, device_id=where, device_id_type=MESH
        )

    small = [
        pltpu.make_async_copy(src, dst, ld.at[9 + n])
        for n, (src, dst) in enumerate(
            [(vconv, cv), (bconv, bcv), (sbias, sb), (lrate, lr), (gain, gn)]
        )
    ]
    load_b = pltpu.make_async_copy(bw, bwv, ld.at[0])
    load_s = pltpu.make_async_copy(sw, swv, ld.at[1])
    load_v0 = pltpu.make_async_copy(vw.at[:, 0:128], w.at[:, 128:256], ld.at[2])
    load_v1 = pltpu.make_async_copy(vw.at[:, 128:CI], w.at[:, 256:768], ld.at[7])
    load_g = pltpu.make_async_copy(gw, w.at[:, 768:1408], ld.at[8])

    def load_h(i):
        s, h = i // 2, i % 2
        return pltpu.make_async_copy(
            hid.at[s, pl.ds(256 * h, 256)], hx.at[s, pl.ds(PAD + 256 * h, 256)], ld.at[3 + i]
        )

    load_b.start()
    load_s.start()
    for copy in small:
        copy.start()
    load_v0.start()
    for i in range(4):
        load_h(i).start()
    load_v1.start()
    load_g.start()

    barrier = pltpu.get_barrier_semaphore()

    def greet_seq(r, _):
        pl.semaphore_signal(
            barrier, inc=1, device_id={"seq": (me + r) & (NS - 1), "tp": z}, device_id_type=MESH
        )
        return 0

    def greet_tp(r, _):
        pl.semaphore_signal(
            barrier, inc=1, device_id={"seq": me, "tp": (z + r) & (NZ - 1)}, device_id_type=MESH
        )
        return 0

    lax.fori_loop(1, NS, greet_seq, 0)
    lax.fori_loop(1, NZ, greet_tp, 0)

    row = lax.broadcasted_iota(jnp.int32, (256, CI), 0)
    col = lax.broadcasted_iota(jnp.int32, (256, CI), 1)
    ee[...] = jnp.where((row & 127) == HL + (col >> 6), 1.0, 0.0).astype(BF16)
    tri_at = lax.broadcasted_iota(jnp.int32, (Q, Q), 0) >= lax.broadcasted_iota(
        jnp.int32, (Q, Q), 1
    )
    tri = jnp.where(tri_at, 1.0, 0.0).astype(BF16)
    prm[...] = jnp.zeros((8, 128), F32)
    dsum[...] = jnp.zeros((8, 128), F32)
    for s in range(2):
        hx[s, 0:8, :] = jnp.zeros((8, D), BF16)

    @pl.when(me == 0)
    def _():
        for s in range(2):
            hx[s, 8:16, :] = jnp.zeros((8, D), BF16)

    for copy in small:
        copy.wait()
    prm[0:1, HL : HL + HEADS] = sb[...]
    prm[1:2, HL : HL + HEADS] = lr[...]
    for k in range(4):
        for h in range(2):
            taps = bcv[k : k + 1, 128 * h : 128 * h + 128]
            tap[2 * k + h] = jnp.broadcast_to(taps, (128, 128)).T
    load_b.wait()
    load_s.wait()
    for n in range(D // 128):
        lanes = slice(128 * n, 128 * n + 128)
        both = jnp.concatenate(
            [bwv[:, lanes].astype(F32), swv[:, lanes].astype(F32), jnp.zeros((86, 128), F32)], axis=0
        )
        w[lanes, 0:128] = both.T.astype(BF16)
    load_v0.wait()

    def first(s):
        for h in range(2):
            load_h(2 * s + h).wait()
            at = 256 * h
            got = dot(hx[s, PAD + at : PAD + at + 256, :], w[:, 0:256])
            bs[s, at : at + 256, :] = got[:, 0:128]
            vp[s, 0, PAD + at : PAD + at + 256, :] = got[:, 128:256]
        for b in range(NB):
            turned = bs[s, Q * b : Q * b + Q, :].T
            bct[s, z, :, Q * b : Q * b + Q] = turned[0:32, :].astype(BF16)

    def piece(p, owner, peer, n):
        part = bct.at[p, owner] if p < 2 else bhl.at[owner]
        return remote(part, part, bsend.at[p, n], brecv.at[p, owner], tp=peer)

    def away(n):
        return (z + n) & (NZ - 1)

    near = ((2, 0), (-2, 1), (1, 2), (-1, 3))

    def passed_on(p):
        turns = [(-2, 1, 4), (2, -1, 5)]
        return turns + [(-2, 2, 6) if p != 1 else (2, -2, 6)]

    def send_piece(p):
        for step, n in near:
            piece(p, z, away(step), n).start()

    def pass_piece(p):
        for step in (-2, 2):
            piece(p, away(step), away(step), 0).wait_recv()
        for owner, target, n in passed_on(p):
            piece(p, away(owner), away(target), n).start()

    def rest_of_piece(p):
        for step in (-1, 1, -3, 3, 4):
            piece(p, away(step), away(step), 0).wait_recv()

    first(0)
    pl.semaphore_wait(barrier, NS - 1 + NZ - 1)
    send_piece(0)
    first(1)
    send_piece(1)

    def halo():
        return remote(hx.at[:, 520:528], hx.at[:, 8:16], hs, hr, seq=(me + 1) & (NS - 1))

    @pl.when(me < NS - 1)
    def _():
        halo().start()

    lane = lax.broadcasted_iota(jnp.int32, (LEN, 128), 1)
    is_head = (lane >= HL) & (lane < HL + HEADS)
    rate = jnp.exp(prm[1:2, :])

    def steps(s):
        x = bs[s] + prm[0:1, :]
        size = jnp.maximum(x, 0.0) + jnp.log1p(jnp.exp(-jnp.abs(x)))
        size = jnp.where(is_head, size, 0.0)
        parts = split(-size * rate)
        so_far = jnp.zeros((1, 128), F32)
        halves, ahead, off = [], [], []
        for b in range(NB):
            sums = dot(tri, parts[Q * b : Q * b + Q, :])
            cum = sums[:, 0:128] + sums[:, 128:256]
            total = cum[Q - 1 : Q, :]
            mid = 0.5 * total
            off.append(cum - mid)
            halves.append(jnp.exp(mid))
            ahead.append(jnp.exp(so_far + mid))
            so_far = so_far + total
        off = jnp.concatenate(off, axis=0)
        av[s] = dot(split(size * jnp.exp(-off)), ee[...])
        ev[s] = dot(split(jnp.exp(off)), ee[...])
        rows = jnp.concatenate(halves + ahead + [jnp.zeros((8, 128), F32)], axis=0)
        rx[s] = dot(split(rows), ee[...])[0:8, :]
        dsum[s : s + 1, :] = so_far

    steps(0)
    steps(1)

    y, x = lax.div(chip, 4), chip & 3
    reach = [0, 1, 2, 1]
    offsets = sorted(
        ((dy, dx) for dy in range(4) for dx in range(4)), key=lambda o: -reach[o[0]] - reach[o[1]]
    )
    chips = [(((y + dy) & 3) * 4 + ((x + dx) & 3), (dy, dx) == (0, 0)) for dy, dx in offsets]
    others = [2 * c + n for c, own in chips for n in range(2) if not own] + [me + 1 - 2 * core]

    def decay(owner, peer):
        src = dsum if owner is None else dall.at[owner]
        slot = me if owner is None else owner
        return remote(src, dall.at[slot], dsend.at[peer], drecv.at[slot], seq=peer)

    for peer in others:
        decay(None, peer).start()
    dall[me] = dsum[...]
    pass_piece(0)

    @pl.when(me > 0)
    def _():
        halo().wait_recv()

    both = jnp.concatenate([hx[0, 8:16, :], hx[1, 8:16, :]], axis=0)
    got = dot(both, w[:, 0:256])
    for s in range(2):
        vp[s, 0, 8:16, :] = got[8 * s : 8 * s + 8, 128:256]
    gap = jnp.zeros((56, 128), F32)
    tail = jnp.concatenate([gap, got[8:16, 0:128], gap, got[0:8, 0:128]], axis=0).T
    bhl[z] = tail[0:32, :].astype(BF16)
    send_piece(2)

    load_v1.wait()

    def value(s):
        for at in (0, 1):
            got = dot(hx[s], w[:, 256 + 256 * at : 512 + 256 * at])
            vp[s, 1 + 2 * at] = got[:, 0:128]
            vp[s, 2 + 2 * at] = got[:, 128:256]
        for b in range(NB):
            for c in range(5):
                lanes = slice(128 * c, 128 * c + 128)
                mixed = None
                for k in range(4):
                    at = 13 + k + Q * b
                    term = cv[k : k + 1, lanes] * vp[s, c, at : at + Q, :]
                    mixed = term if mixed is None else mixed + term
                here = (s, slice(Q * b, Q * b + Q), lanes)
                vv[here] = (silu(mixed) * av[here]).astype(BF16)

    value(0)
    pass_piece(1)
    pass_piece(2)
    value(1)

    def mix(s, h):
        ahead = bhl[4 * h : 4 * h + 4].astype(F32).reshape(128, 128)
        if s == 1:
            ahead = pltpu.roll(ahead, 64, 1)
        x = bct[s, 4 * h : 4 * h + 4].astype(F32).reshape(128, LEN)
        x = jnp.concatenate([ahead, x], axis=1)
        turned = [pltpu.roll(x, 3 - k, 1) for k in range(3)] + [x]
        blocks = []
        for b in range(NB):
            lanes = slice(128 + Q * b, 256 + Q * b)
            mixed = tap[h] * turned[0][:, lanes]
            for k in range(1, 4):
                mixed = mixed + tap[2 * k + h] * turned[k][:, lanes]
            blocks.append(silu(mixed))
        return blocks

    def first_hop(source, k, s):
        owner = 2 * k + s
        return remote(st.at[s, k], p1.at[source], s1.at[owner], r1.at[source], seq=owner)

    def states(s):
        for b, block in enumerate(mix(s, 0)):
            bmat[s, :, Q * b : Q * b + Q] = block.astype(BF16)
        state = None
        for b in range(NB):
            half = rx[s, b : b + 1, :]
            added = dot(bmat[s, :, Q * b : Q * b + Q], vv[s, Q * b : Q * b + Q, :]) * half
            if state is None:
                sbl[s, b] = jnp.zeros((128, CI), BF16)
                state = added
            else:
                lifted = state * half
                sbl[s, b] = lifted.astype(BF16)
                state = lifted * half + added
        for k in range(16):
            st[s, k] = state[8 * k : 8 * k + 8, :].astype(BF16)
        for k, own in chips:
            if own:

                @pl.when(core != s)
                def _():
                    first_hop(me, k, s).start()

            else:
                first_hop(me, k, s).start()

    rest_of_piece(2)
    for s in range(2):
        rest_of_piece(s)
        states(s)
    p1[me] = st[core, chip]

    def within(s):
        for b, block in enumerate(mix(s, 1)):
            cmat[s, Q * b : Q * b + Q, :] = block.T.astype(BF16)
        for b in range(NB):
            rows = slice(Q * b, Q * b + Q)
            c_rows = cmat[s, rows, :]
            scores = dot(c_rows, bmat[s, :, rows])
            scores = jnp.where(tri_at, scores, 0.0).astype(BF16)
            left = jnp.concatenate([scores, c_rows], axis=1)
            right = jnp.concatenate([vv[s, rows, :], sbl[s, b]], axis=0)
            g[s, rows, :] = dot(left, right)

    within(0)
    within(1)

    for peer in others:
        decay(peer, peer).wait_recv()

    def pick(j, _):
        dxl[pl.ds(j, 1), :] = dall[j, pl.ds(core, 1), :]
        return 0

    lax.fori_loop(0, NS, pick, 0, unroll=True)
    dx[...] = dot(split(jnp.exp(dxl[...])), ee[...])

    for peer in others:
        first_hop(peer, chip, core).wait_recv()
    so_far = jnp.zeros((8, CI), F32)
    for j in range(NS):
        po[j] = so_far.astype(BF16)
        so_far = so_far * dx[j : j + 1, :] + p1[j].astype(F32)

    def second_hop(target, source):
        slot = pin.at[source & 1, lax.div(source, 2)]
        return remote(po.at[target], slot, s2.at[target], r2.at[source], seq=target)

    for peer in others:
        second_hop(peer, me).start()
    pin[core, chip] = po[me]

    load_g.wait()

    def gate(s, _):
        for at, wide in ((0, 256), (256, 256), (512, 128)):
            got = dot(hx[s, PAD : PAD + LEN, :], w[:, 768 + at : 768 + at + wide])
            fg[s, :, at : at + wide] = silu(got) * ev[s, :, at : at + wide]
        return 0

    lax.fori_loop(0, 2, gate, 0)

    ones = jnp.ones((16, 128), BF16)
    at_row = lax.broadcasted_iota(jnp.int32, (8, 128), 0)
    squares = jnp.zeros((8, 128), F32)
    for peer in others:
        second_hop(peer, peer).wait_recv()
    for s in range(2):
        arrived = pin[s].astype(F32).reshape(128, CI).astype(BF16)
        given = dot(cmat[s], arrived)
        for b in range(NB):
            rows = slice(Q * b, Q * b + Q)
            gated = fg[s, rows, :] * (g[s, rows, :] + given[rows] * rx[s, 4 + b : 5 + b, :])
            g[s, rows, :] = gated
            sq = gated * gated
            sq = sum(sq[:, 128 * c : 128 * c + 128] for c in range(1, 5)) + sq[:, 0:128]
            summed = lax.dot_general(
                ones, sq.astype(BF16), (((1,), (1,)), ((), ())), preferred_element_type=F32
            )[0:8, :]
            squares = jnp.where(at_row == 4 * s + b, summed, squares)
    ssm[...] = squares

    def total_sq(owner, peer):
        return remote(ssm, ssa.at[owner], zs.at[peer], zr.at[owner], tp=peer)

    for step in (4, 3, -3, 2, -2, 1, -1):
        total_sq(z, away(step)).start()
    ssa[z] = ssm[...]
    for step in (4, 3, -3, 2, -2, 1, -1):
        total_sq(away(step), away(step)).wait_recv()
    scale = lax.rsqrt(jnp.sum(ssa[...], axis=0) * (1.0 / DI) + EPS)
    gains = gn[...].reshape(1, CI)
    for s in range(2):
        for b in range(NB):
            rows = slice(Q * b, Q * b + Q)
            by_token = jnp.broadcast_to(scale[4 * s + b : 4 * s + b + 1, :], (128, 128)).T
            for c in range(5):
                lanes = slice(128 * c, 128 * c + 128)
                osc[s, rows, lanes] = (g[s, rows, lanes] * by_token * gains[:, lanes]).astype(BF16)
        pltpu.make_async_copy(osc.at[s], out.at[s], lo.at[s]).start()

    for p in range(3):
        for step, n in near:
            piece(p, z, away(step), n).wait_send()
        for owner, target, n in passed_on(p):
            piece(p, away(owner), away(target), n).wait_send()
    for step in range(1, NZ):
        total_sq(z, away(step)).wait_send()

    def sent_seq(r, _):
        peer = (me + r) & (NS - 1)
        decay(None, peer).wait_send()
        first_hop(me, lax.div(peer, 2), peer & 1).wait_send()
        second_hop(peer, me).wait_send()
        return 0

    lax.fori_loop(1, NS, sent_seq, 0)
    @pl.when(me < NS - 1)
    def _():
        halo().wait_send()

    for s in range(2):
        pltpu.make_async_copy(osc.at[s], out.at[s], lo.at[s]).wait()


def on_device(hid, gw, vw, bw, sw, vconv, bconv, sbias, lrate, gain):
    dma = pltpu.SemaphoreType.DMA
    vmem = pltpu.VMEM
    any_space = pl.BlockSpec(memory_space=pl.ANY)
    scratch = [
        vmem((2, PAD + LEN, D), BF16),
        vmem((D, 1408), BF16),
        vmem((32, D), BF16),
        vmem((HEADS, D), BF16),
        vmem((4, CI), F32),
        vmem((4, 256), F32),
        vmem((1, HEADS), F32),
        vmem((1, HEADS), F32),
        vmem((CI,), F32),
        vmem((8, 128), F32),
        vmem((8, 128, 128), F32),
        vmem((256, CI), BF16),
        vmem((2, LEN, 128), F32),
        vmem((2, 5, PAD + LEN, 128), F32),
        vmem((2, NZ, 32, LEN), BF16),
        vmem((2, LEN, 128), BF16),
        vmem((2, 128, LEN), BF16),
        vmem((2, LEN, CI), F32),
        vmem((2, LEN, CI), F32),
        vmem((2, LEN, CI), F32),
        vmem((2, LEN, CI), F32),
        vmem((2, 8, CI), F32),
        vmem((8, 128), F32),
        vmem((NS, 8, 128), F32),
        vmem((NS, 128), F32),
        vmem((NS, CI), F32),
        vmem((NZ, 32, 128), BF16),
        vmem((2, LEN, CI), BF16),
        vmem((2, NB, 128, CI), BF16),
        vmem((2, 16, 8, CI), BF16),
        vmem((NS, 8, CI), BF16),
        vmem((NS, 8, CI), BF16),
        vmem((2, 16, 8, CI), BF16),
        vmem((8, 128), F32),
        vmem((NZ, 8, 128), F32),
        vmem((2, LEN, CI), BF16),
        dma((14,)),
        dma((2,)),
        dma,
        dma,
        dma((3, 7)),
        dma((3, NZ)),
        dma((NS,)),
        dma((NS,)),
        dma((NS,)),
        dma((NS,)),
        dma((NS,)),
        dma((NS,)),
        dma((NZ,)),
        dma((NZ,)),
    ]
    return pl.pallas_call(
        kernel,
        out_shape=jax.ShapeDtypeStruct((2, LEN, CI), BF16),
        in_specs=[any_space] * 10,
        out_specs=any_space,
        scratch_shapes=scratch,
        compiler_params=pltpu.CompilerParams(
            collective_id=0, has_side_effects=True, vmem_limit_bytes=56 * 2**20
        ),
    )(
        hid, gw, vw, bw.T, sw.T, vconv, bconv,
        sbias.reshape(1, HEADS), lrate.reshape(1, HEADS), gain,
    )


def solution(mesh):
    placed = (
        P(None, "seq", None),
        P(None, "tp"),
        P(None, "tp"),
        P(None, "tp"),
        P(None, "tp"),
        P(None, "tp"),
        P(),
        P("tp"),
        P("tp"),
        P("tp"),
    )
    return jax.shard_map(
        on_device, mesh=mesh, in_specs=placed, out_specs=P(None, "seq", "tp"), check_vma=False
    )
```

time: 59.3 us -> 49 us (0.83)
  local copies, waits for them, and re-layouts: 7.8 us -> 2.49 us
  Pallas kernels: 51.3 us -> 46.4 us
    pallas_call x1, Pallas kernels: 51.3 us -> 46.4 us  [on_device(): pl.pallas_call(kernel, out_shape=jax.ShapeDtypeStruct((2, LEN, CI), BF16)...]
    unnamed x3 -> x1, local copies, waits for them, and re-layouts: 6.52 us -> 2.49 us
    reshape x1 -> x0, local copies, waits for them, and re-layouts: 1.28 us -> none  [on_device(): gain.reshape(1, CI)]
where the time goes in v2:
time: 49 us; the launch traced here: 48.9 us
  Pallas kernels  46.4 us (95%)
  local copies, waits for them, and re-layouts  2.49 us (5%)
    pallas_call x1, Pallas kernels, on_device(): pl.pallas_call(kernel, out_shape=jax.ShapeDtypeStruct((2, LEN, CI), BF16)...  46.4 us
    unnamed x1, local copies, waits for them, and re-layouts  2.49 us

profile of v2, /device:TPU:1, one launch (start us, length us, event | category | flops | bytes accessed | tf_op | source)
XLA Modules:
  0.0 48.9 jit_solution(5113543176486835292)
XLA Ops:
  0.0 46.4 %shard_map.100 = bf16[2,512,640]{2,1,0:T(8,128)(2,1)} custom-call(bf16[2,512,2560]{2,1,0:T(8,128)(2,1)} %hid.1, bf16[2560,640]{1,0:T(8,128)(2,1)} %gw.1, bf16[2560,640]{1,0:T(8,128)(2,1)} %vw.1, bf16[32,2560]{1,0:T(8,128)(2,1)} %bitcast.4, bf16[10,2560]{1,0:T(8,128)(2,1)} %bitcast.5, f32[4,640]{1,0:T(4,128)} %vconv.1, f32[4,256]{1,0:T(4,128)} %bconv.1, ...), custom_call_target="tpu_custom_call" | custom-call | tf_op jit(solution)/shard_map/pallas_call | solution.py:489
  46.4 2.5 %copy.12 = bf16[2,512,640]{2,1,0:T(8,128)(2,1)} copy(bf16[2,512,640]{2,1,0:T(8,128)(2,1)} %shard_map.100) | data formatting | bytes 2621440

commit v3 on v2

--- a/solution.py
+++ b/solution.py
@@ -36,10 +36,10 @@
 
 
 def kernel(
-    hid, gw, vw, bw, sw, vconv, bconv, sbias, lrate, gain, out,
+    hid, gw, vw, bw, sw, vconv, bconv, sbias, lrate, gain, out, rms,
     hx, w, bwv, swv, cv, bcv, sb, lr, gn, prm, tap, ee, bs, vp, bct, cmat, bmat,
-    av, ev, fg, g, rx, dsum, dall, dxl, dx, bhl, vv, sbl, st, p1, po, pin, ssm, ssa, osc,
-    ld, lo, hs, hr, bsend, brecv, dsend, drecv, s1, r1, s2, r2, zs, zr,
+    av, ev, fg, g, rx, dsum, dall, dxl, dx, bhl, vv, sbl, st, p1, po, pin, ssm, ssa,
+    ld, hs, hr, bsend, brecv, dsend, drecv, s1, r1, s2, r2, zs, zr,
 ):
     me, z = lax.axis_index("seq"), lax.axis_index("tp")
     core, chip = me & 1, lax.div(me, 2)
@@ -393,18 +393,12 @@
     for step in (4, 3, -3, 2, -2, 1, -1):
         total_sq(z, away(step)).start()
     ssa[z] = ssm[...]
+    gains = gn[...].reshape(1, CI)
+    for s in range(2):
+        out[s] = g[s] * gains
     for step in (4, 3, -3, 2, -2, 1, -1):
         total_sq(away(step), away(step)).wait_recv()
-    scale = lax.rsqrt(jnp.sum(ssa[...], axis=0) * (1.0 / DI) + EPS)
-    gains = gn[...].reshape(1, CI)
-    for s in range(2):
-        for b in range(NB):
-            rows = slice(Q * b, Q * b + Q)
-            by_token = jnp.broadcast_to(scale[4 * s + b : 4 * s + b + 1, :], (128, 128)).T
-            for c in range(5):
-                lanes = slice(128 * c, 128 * c + 128)
-                osc[s, rows, lanes] = (g[s, rows, lanes] * by_token * gains[:, lanes]).astype(BF16)
-        pltpu.make_async_copy(osc.at[s], out.at[s], lo.at[s]).start()
+    rms[...] = lax.rsqrt(jnp.sum(ssa[...], axis=0) * (1.0 / DI) + EPS)
 
     for p in range(3):
         for step, n in near:
@@ -426,8 +420,21 @@
     def _():
         halo().wait_send()
 
+
+def scaled(gated, rms, out, osc, sems):
+    copies = []
     for s in range(2):
-        pltpu.make_async_copy(osc.at[s], out.at[s], lo.at[s]).wait()
+        for b in range(NB):
+            n = NB * s + b
+            rows = slice(Q * b, Q * b + Q)
+            by_token = jnp.broadcast_to(rms[n : n + 1, :], (128, 128)).T
+            for c in range(5):
+                lanes = slice(128 * c, 128 * c + 128)
+                osc[s, rows, lanes] = (gated[s, rows, lanes] * by_token).astype(BF16)
+            copies.append(pltpu.make_async_copy(osc.at[s, rows], out.at[s, rows], sems.at[n]))
+            copies[-1].start()
+    for copy in copies:
+        copy.wait()
 
 
 def on_device(hid, gw, vw, bw, sw, vconv, bconv, sbias, lrate, gain):
@@ -470,9 +477,7 @@
         vmem((2, 16, 8, CI), BF16),
         vmem((8, 128), F32),
         vmem((NZ, 8, 128), F32),
-        vmem((2, LEN, CI), BF16),
         dma((14,)),
-        dma((2,)),
         dma,
         dma,
         dma((3, 7)),
@@ -486,11 +491,12 @@
         dma((NZ,)),
         dma((NZ,)),
     ]
-    return pl.pallas_call(
+    in_vmem = pl.BlockSpec(memory_space=vmem)
+    gated, rms = pl.pallas_call(
         kernel,
-        out_shape=jax.ShapeDtypeStruct((2, LEN, CI), BF16),
+        out_shape=(vmem((2, LEN, CI), F32), vmem((8, 128), F32)),
         in_specs=[any_space] * 10,
-        out_specs=any_space,
+        out_specs=(in_vmem, in_vmem),
         scratch_shapes=scratch,
         compiler_params=pltpu.CompilerParams(
             collective_id=0, has_side_effects=True, vmem_limit_bytes=56 * 2**20
@@ -499,6 +505,13 @@
         hid, gw, vw, bw.T, sw.T, vconv, bconv,
         sbias.reshape(1, HEADS), lrate.reshape(1, HEADS), gain,
     )
+    return pl.pallas_call(
+        scaled,
+        out_shape=jax.ShapeDtypeStruct((2, LEN, CI), BF16),
+        in_specs=[in_vmem, in_vmem],
+        out_specs=any_space,
+        scratch_shapes=[vmem((2, LEN, CI), BF16), dma((2 * NB,))],
+    )(*(pltpu.with_memory_space_constraint(x, vmem) for x in (gated, rms)))
 
 
 def solution(mesh):

time: 49 us -> 47.1 us (0.961)
  local copies, waits for them, and re-layouts: 2.49 us -> 0 us
  Pallas kernels: 46.4 us -> 46.9 us
    unnamed x1 -> x0, local copies, waits for them, and re-layouts: 2.49 us -> none
    pallas_call x1 -> x2, Pallas kernels: 46.4 us -> 46.9 us  [the longest x1 45.7 us: on_device(): pl.pallas_call(kernel, out_shape=(vmem((2, LEN, CI), F32), vmem((8, 128),...]
where the time goes in v3:
time: 47.1 us; the launch traced here: 47 us
  Pallas kernels  46.9 us (100%)
    pallas_call x1, Pallas kernels, on_device(): pl.pallas_call(kernel, out_shape=(vmem((2, LEN, CI), F32), vmem((8, 128),...  45.7 us
    pallas_call x1, Pallas kernels, on_device(): pl.pallas_call(scaled, out_shape=jax.ShapeDtypeStruct((2, LEN, CI), BF16)...  1.22 us

profile of v3, /device:TPU:1, one launch (start us, length us, event | category | flops | bytes accessed | tf_op | source)
XLA Modules:
  0.0 47.0 jit_solution(5557597790791538898)
XLA Ops:
  0.0 45.7 %shard_map.100 = (f32[2,512,640]{2,1,0:T(8,128)S(1)}, f32[8,128]{1,0:T(8,128)S(1)}) custom-call(bf16[2,512,2560]{2,1,0:T(8,128)(2,1)} %hid.1, bf16[2560,640]{1,0:T(8,128)(2,1)} %gw.1, bf16[2560,640]{1,0:T(8,128)(2,1)} %vw.1, bf16[32,2560]{1,0:T(8,128)(2,1)} %bitcast.4, bf16[10,2560]{1,0:T(8,128)(2,1)} %bitcast.5, f32[4,640]{1,0:T(4,128)} %vconv.1, ...), custom_call_target="tpu_custom_call" | custom-call | tf_op jit(solution)/shard_map/pallas_call | solution.py:495
  45.7 1.2 %shard_map.101 = bf16[2,512,640]{2,1,0:T(8,128)(2,1)} custom-call(f32[2,512,640]{2,1,0:T(8,128)S(1)} %get-tuple-element.7.gated, f32[8,128]{1,0:T(8,128)S(1)} %get-tuple-element.8.rms), custom_call_target="tpu_custom_call" | custom-call | tf_op jit(solution)/shard_map/pallas_call | solution.py:508

commit v4 on v3

--- a/solution.py
+++ b/solution.py
@@ -38,11 +38,12 @@
 def kernel(
     hid, gw, vw, bw, sw, vconv, bconv, sbias, lrate, gain, out, rms,
     hx, w, bwv, swv, cv, bcv, sb, lr, gn, prm, tap, ee, bs, vp, bct, cmat, bmat,
-    av, ev, fg, g, rx, dsum, dall, dxl, dx, bhl, vv, sbl, st, p1, po, pin, ssm, ssa,
-    ld, hs, hr, bsend, brecv, dsend, drecv, s1, r1, s2, r2, zs, zr,
+    av, ev, fg, g, rx, dsum, dall, dxl, dx, bhl, vv, sbl, st, so, agg, p1, po, pin, ssm, ssa,
+    ld, hs, hr, bsend, brecv, dsend, drecv, s1, r1, s2, r2, zs, zr, cs, cr,
 ):
     me, z = lax.axis_index("seq"), lax.axis_index("tp")
     core, chip = me & 1, lax.div(me, 2)
+    early, late = 1 - core, core
 
     def remote(src, dst, ss, rs, seq=None, tp=None):
         where = {"seq": me if seq is None else seq, "tp": z if tp is None else tp}
@@ -62,10 +63,9 @@
     load_v1 = pltpu.make_async_copy(vw.at[:, 128:CI], w.at[:, 256:768], ld.at[7])
     load_g = pltpu.make_async_copy(gw, w.at[:, 768:1408], ld.at[8])
 
-    def load_h(i):
-        s, h = i // 2, i % 2
+    def load_h(s, h):
         return pltpu.make_async_copy(
-            hid.at[s, pl.ds(256 * h, 256)], hx.at[s, pl.ds(PAD + 256 * h, 256)], ld.at[3 + i]
+            hid.at[s, pl.ds(256 * h, 256)], hx.at[s, pl.ds(PAD + 256 * h, 256)], ld.at[3 + 2 * s + h]
         )
 
     load_b.start()
@@ -73,8 +73,9 @@
     for copy in small:
         copy.start()
     load_v0.start()
-    for i in range(4):
-        load_h(i).start()
+    for s in (early, late):
+        for h in range(2):
+            load_h(s, h).start()
     load_v1.start()
     load_g.start()
 
@@ -132,7 +133,7 @@
 
     def first(s):
         for h in range(2):
-            load_h(2 * s + h).wait()
+            load_h(s, h).wait()
             at = 256 * h
             got = dot(hx[s, PAD + at : PAD + at + 256, :], w[:, 0:256])
             bs[s, at : at + 256, :] = got[:, 0:128]
@@ -142,7 +143,7 @@
             bct[s, z, :, Q * b : Q * b + Q] = turned[0:32, :].astype(BF16)
 
     def piece(p, owner, peer, n):
-        part = bct.at[p, owner] if p < 2 else bhl.at[owner]
+        part = bct.at[(early, late)[p], owner] if p < 2 else bhl.at[owner]
         return remote(part, part, bsend.at[p, n], brecv.at[p, owner], tp=peer)
 
     def away(n):
@@ -168,10 +169,10 @@
         for step in (-1, 1, -3, 3, 4):
             piece(p, away(step), away(step), 0).wait_recv()
 
-    first(0)
+    first(early)
     pl.semaphore_wait(barrier, NS - 1 + NZ - 1)
     send_piece(0)
-    first(1)
+    first(late)
     send_piece(1)
 
     def halo():
@@ -206,10 +207,10 @@
         ev[s] = dot(split(jnp.exp(off)), ee[...])
         rows = jnp.concatenate(halves + ahead + [jnp.zeros((8, 128), F32)], axis=0)
         rx[s] = dot(split(rows), ee[...])[0:8, :]
-        dsum[s : s + 1, :] = so_far
-
-    steps(0)
-    steps(1)
+        dsum[pl.ds(s, 1), :] = so_far
+
+    steps(early)
+    steps(late)
 
     y, x = lax.div(chip, 4), chip & 3
     reach = [0, 1, 2, 1]
@@ -244,31 +245,36 @@
 
     load_v1.wait()
 
-    def value(s):
-        for at in (0, 1):
-            got = dot(hx[s], w[:, 256 + 256 * at : 512 + 256 * at])
-            vp[s, 1 + 2 * at] = got[:, 0:128]
-            vp[s, 2 + 2 * at] = got[:, 128:256]
-        for b in range(NB):
-            for c in range(5):
-                lanes = slice(128 * c, 128 * c + 128)
-                mixed = None
-                for k in range(4):
-                    at = 13 + k + Q * b
-                    term = cv[k : k + 1, lanes] * vp[s, c, at : at + Q, :]
-                    mixed = term if mixed is None else mixed + term
-                here = (s, slice(Q * b, Q * b + Q), lanes)
-                vv[here] = (silu(mixed) * av[here]).astype(BF16)
-
-    value(0)
+    def project(s, at):
+        got = dot(hx[s], w[:, 256 + 256 * at : 512 + 256 * at])
+        vp[s, 1 + 2 * at] = got[:, 0:128]
+        vp[s, 2 + 2 * at] = got[:, 128:256]
+
+    def value(s, b):
+        for c in range(5):
+            lanes = slice(128 * c, 128 * c + 128)
+            mixed = None
+            for k in range(4):
+                at = 13 + k + Q * b
+                term = cv[k : k + 1, lanes] * vp[s, c, at : at + Q, :]
+                mixed = term if mixed is None else mixed + term
+            here = (s, slice(Q * b, Q * b + Q), lanes)
+            vv[here] = (silu(mixed) * av[here]).astype(BF16)
+
+    project(early, 0)
+    project(early, 1)
+    for at in range(2):
+        project(late, at)
+        value(early, 2 * at)
+        value(early, 2 * at + 1)
     pass_piece(1)
     pass_piece(2)
-    value(1)
+    for b in range(NB):
+        value(late, b)
 
     def mix(s, h):
         ahead = bhl[4 * h : 4 * h + 4].astype(F32).reshape(128, 128)
-        if s == 1:
-            ahead = pltpu.roll(ahead, 64, 1)
+        ahead = jnp.where(s == 1, pltpu.roll(ahead, 64, 1), ahead)
         x = bct[s, 4 * h : 4 * h + 4].astype(F32).reshape(128, LEN)
         x = jnp.concatenate([ahead, x], axis=1)
         turned = [pltpu.roll(x, 3 - k, 1) for k in range(3)] + [x]
@@ -281,9 +287,18 @@
             blocks.append(silu(mixed))
         return blocks
 
-    def first_hop(source, k, s):
-        owner = 2 * k + s
-        return remote(st.at[s, k], p1.at[source], s1.at[owner], r1.at[source], seq=owner)
+    for peer in others:
+        decay(peer, peer).wait_recv()
+
+    def pick(j, _):
+        dxl[pl.ds(j, 1), :] = dall[2 * j, pl.ds(core, 1), :] + dall[2 * j + 1, pl.ds(core, 1), :]
+        return 0
+
+    lax.fori_loop(0, 16, pick, 0, unroll=True)
+    dxl[16:17, :] = dall[2 * chip + 1, pl.ds(core, 1), :]
+    dxl[24:32, :] = dall[2 * chip]
+    dxl[17:24, :] = jnp.zeros((7, 128), F32)
+    dx[...] = dot(split(jnp.exp(dxl[...])), ee[...])
 
     def states(s):
         for b, block in enumerate(mix(s, 0)):
@@ -301,21 +316,34 @@
                 state = lifted * half + added
         for k in range(16):
             st[s, k] = state[8 * k : 8 * k + 8, :].astype(BF16)
-        for k, own in chips:
-            if own:
-
-                @pl.when(core != s)
-                def _():
-                    first_hop(me, k, s).start()
-
-            else:
-                first_hop(me, k, s).start()
+
+    def across(s, n):
+        return remote(st.at[s], so.at[s], cs.at[n], cr.at[n], seq=me + 1 - 2 * core)
 
     rest_of_piece(2)
-    for s in range(2):
-        rest_of_piece(s)
-        states(s)
-    p1[me] = st[core, chip]
+    rest_of_piece(0)
+    states(early)
+    across(early, 0).start()
+    rest_of_piece(1)
+    states(late)
+
+    @pl.when(core == 0)
+    def _():
+        across(0, 1).start()
+
+    def first_hop(source, k):
+        return remote(agg.at[k], p1.at[source], s1.at[k], r1.at[source], seq=2 * k + core)
+
+    across(late, 0).wait_recv()
+    carry = dx[16:17, :]
+    for k, own in chips:
+        mine, other = st[late, k].astype(F32), so[late, k].astype(F32)
+        slab = jnp.where(core == 0, mine, other) * carry + jnp.where(core == 0, other, mine)
+        agg[k] = slab.astype(BF16)
+        if own:
+            p1[k] = agg[k]
+        else:
+            first_hop(chip, k).start()
 
     def within(s):
         for b, block in enumerate(mix(s, 1)):
@@ -329,33 +357,26 @@
             right = jnp.concatenate([vv[s, rows, :], sbl[s, b]], axis=0)
             g[s, rows, :] = dot(left, right)
 
-    within(0)
-    within(1)
-
-    for peer in others:
-        decay(peer, peer).wait_recv()
-
-    def pick(j, _):
-        dxl[pl.ds(j, 1), :] = dall[j, pl.ds(core, 1), :]
-        return 0
-
-    lax.fori_loop(0, NS, pick, 0, unroll=True)
-    dx[...] = dot(split(jnp.exp(dxl[...])), ee[...])
-
-    for peer in others:
-        first_hop(peer, chip, core).wait_recv()
+    within(early)
+    within(late)
+
+    for k, own in chips:
+        if not own:
+            first_hop(k, chip).wait_recv()
     so_far = jnp.zeros((8, CI), F32)
-    for j in range(NS):
+    for j in range(16):
         po[j] = so_far.astype(BF16)
         so_far = so_far * dx[j : j + 1, :] + p1[j].astype(F32)
 
     def second_hop(target, source):
-        slot = pin.at[source & 1, lax.div(source, 2)]
-        return remote(po.at[target], slot, s2.at[target], r2.at[source], seq=target)
-
-    for peer in others:
-        second_hop(peer, me).start()
-    pin[core, chip] = po[me]
+        slot = pin.at[late, source]
+        return remote(po.at[target], slot, s2.at[target], r2.at[source], seq=2 * target + core)
+
+    for k, own in chips:
+        if own:
+            pin[late, k] = po[k]
+        else:
+            second_hop(k, chip).start()
 
     load_g.wait()
 
@@ -370,10 +391,25 @@
     ones = jnp.ones((16, 128), BF16)
     at_row = lax.broadcasted_iota(jnp.int32, (8, 128), 0)
     squares = jnp.zeros((8, 128), F32)
-    for peer in others:
-        second_hop(peer, peer).wait_recv()
-    for s in range(2):
-        arrived = pin[s].astype(F32).reshape(128, CI).astype(BF16)
+    for k, own in chips:
+        if not own:
+            second_hop(k, k).wait_recv()
+
+    def back(s):
+        return remote(pin.at[s], pin.at[s], cs.at[2], cr.at[2], seq=me + 1 - 2 * core)
+
+    back(late).start()
+
+    @pl.when(core == 1)
+    def _():
+        across(0, 1).wait_recv()
+
+    for s in (late, early):
+        if s is early:
+            back(early).wait_recv()
+        arrived = pin[s].astype(F32).reshape(128, CI)
+        moved = arrived * dx[pl.ds(24 + s, 1), :] + so[s].astype(F32).reshape(128, CI)
+        arrived = jnp.where(core == 1, moved, arrived).astype(BF16)
         given = dot(cmat[s], arrived)
         for b in range(NB):
             rows = slice(Q * b, Q * b + Q)
@@ -408,14 +444,19 @@
     for step in range(1, NZ):
         total_sq(z, away(step)).wait_send()
 
-    def sent_seq(r, _):
-        peer = (me + r) & (NS - 1)
+    for peer in others:
         decay(None, peer).wait_send()
-        first_hop(me, lax.div(peer, 2), peer & 1).wait_send()
-        second_hop(peer, me).wait_send()
-        return 0
-
-    lax.fori_loop(1, NS, sent_seq, 0)
+    for k, own in chips:
+        if not own:
+            first_hop(chip, k).wait_send()
+            second_hop(k, chip).wait_send()
+    across(early, 0).wait_send()
+    back(late).wait_send()
+
+    @pl.when(core == 0)
+    def _():
+        across(0, 1).wait_send()
+
     @pl.when(me < NS - 1)
     def _():
         halo().wait_send()
@@ -472,8 +513,10 @@
         vmem((2, LEN, CI), BF16),
         vmem((2, NB, 128, CI), BF16),
         vmem((2, 16, 8, CI), BF16),
-        vmem((NS, 8, CI), BF16),
-        vmem((NS, 8, CI), BF16),
+        vmem((2, 16, 8, CI), BF16),
+        vmem((16, 8, CI), BF16),
+        vmem((16, 8, CI), BF16),
+        vmem((16, 8, CI), BF16),
         vmem((2, 16, 8, CI), BF16),
         vmem((8, 128), F32),
         vmem((NZ, 8, 128), F32),
@@ -484,12 +527,14 @@
         dma((3, NZ)),
         dma((NS,)),
         dma((NS,)),
-        dma((NS,)),
-        dma((NS,)),
-        dma((NS,)),
-        dma((NS,)),
+        dma((16,)),
+        dma((16,)),
+        dma((16,)),
+        dma((16,)),
         dma((NZ,)),
         dma((NZ,)),
+        dma((3,)),
+        dma((3,)),
     ]
     in_vmem = pl.BlockSpec(memory_space=vmem)
     gated, rms = pl.pallas_call(

time: 47.1 us -> 45.5 us (0.966)
  Pallas kernels: 46.9 us -> 45.3 us
    pallas_call x1, Pallas kernels: 45.7 us -> 44 us  [on_device(): pl.pallas_call(kernel, out_shape=(vmem((2, LEN, CI), F32), vmem((8, 128),...]
where the time goes in v4:
time: 45.5 us; the launch traced here: 45.4 us
  Pallas kernels  45.3 us (100%)
    pallas_call x1, Pallas kernels, on_device(): pl.pallas_call(kernel, out_shape=(vmem((2, LEN, CI), F32), vmem((8, 128),...  44 us
    pallas_call x1, Pallas kernels, on_device(): pl.pallas_call(scaled, out_shape=jax.ShapeDtypeStruct((2, LEN, CI), BF16)...  1.22 us

profile of v4, /device:TPU:1, one launch (start us, length us, event | category | flops | bytes accessed | tf_op | source)
XLA Modules:
  0.0 45.4 jit_solution(82956694185500398)
XLA Ops:
  0.0 44.0 %shard_map.100 = (f32[2,512,640]{2,1,0:T(8,128)S(1)}, f32[8,128]{1,0:T(8,128)S(1)}) custom-call(bf16[2,512,2560]{2,1,0:T(8,128)(2,1)} %hid.1, bf16[2560,640]{1,0:T(8,128)(2,1)} %gw.1, bf16[2560,640]{1,0:T(8,128)(2,1)} %vw.1, bf16[32,2560]{1,0:T(8,128)(2,1)} %bitcast.4, bf16[10,2560]{1,0:T(8,128)(2,1)} %bitcast.5, f32[4,640]{1,0:T(4,128)} %vconv.1, ...), custom_call_target="tpu_custom_call" | custom-call | tf_op jit(solution)/shard_map/pallas_call | solution.py:540
  44.0 1.2 %shard_map.101 = bf16[2,512,640]{2,1,0:T(8,128)(2,1)} custom-call(f32[2,512,640]{2,1,0:T(8,128)S(1)} %get-tuple-element.7.gated, f32[8,128]{1,0:T(8,128)S(1)} %get-tuple-element.8.rms), custom_call_target="tpu_custom_call" | custom-call | tf_op jit(solution)/shard_map/pallas_call | solution.py:553

commit v5 on v4

--- a/solution.py
+++ b/solution.py
@@ -38,7 +38,7 @@
 def kernel(
     hid, gw, vw, bw, sw, vconv, bconv, sbias, lrate, gain, out, rms,
     hx, w, bwv, swv, cv, bcv, sb, lr, gn, prm, tap, ee, bs, vp, bct, cmat, bmat,
-    av, ev, fg, g, rx, dsum, dall, dxl, dx, bhl, vv, sbl, st, so, agg, p1, po, pin, ssm, ssa,
+    av, es, fg, g, rx, dsum, dall, dxl, dx, bhl, vv, sbl, st, so, agg, p1, po, pin, ssm, ssa,
     ld, hs, hr, bsend, brecv, dsend, drecv, s1, r1, s2, r2, zs, zr, cs, cr,
 ):
     me, z = lax.axis_index("seq"), lax.axis_index("tp")
@@ -133,7 +133,8 @@
 
     def first(s):
         for h in range(2):
-            load_h(s, h).wait()
+            if s is early:
+                load_h(s, h).wait()
             at = 256 * h
             got = dot(hx[s, PAD + at : PAD + at + 256, :], w[:, 0:256])
             bs[s, at : at + 256, :] = got[:, 0:128]
@@ -150,37 +151,53 @@
         return (z + n) & (NZ - 1)
 
     near = ((2, 0), (-2, 1), (1, 2), (-1, 3))
-
-    def passed_on(p):
-        turns = [(-2, 1, 4), (2, -1, 5)]
-        return turns + [(-2, 2, 6) if p != 1 else (2, -2, 6)]
+    far_first = (4, 3, -3, 2, -2, 1, -1)
+    to_b = jnp.where((z >= 2) & (z < 6), 1, -1)
 
     def send_piece(p):
         for step, n in near:
             piece(p, z, away(step), n).start()
 
-    def pass_piece(p):
-        for step in (-2, 2):
-            piece(p, away(step), away(step), 0).wait_recv()
-        for owner, target, n in passed_on(p):
-            piece(p, away(owner), away(target), n).start()
-
-    def rest_of_piece(p):
-        for step in (-1, 1, -3, 3, 4):
-            piece(p, away(step), away(step), 0).wait_recv()
+    def passed_on(p, way, act):
+        owner = away(-2 * way)
+        n = jnp.where(way > 0, 4, 5)
+        act(piece(p, owner, away(way), n))
+
+        @pl.when(way == (-1 if p else 1))
+        def _():
+            act(piece(p, owner, away(2 * way), 6))
+
+    def pass_piece(p, way):
+        owner = away(-2 * way)
+        piece(p, owner, owner, 0).wait_recv()
+        passed_on(p, way, lambda copy: copy.start())
+
+    def rest_of_piece(p, owners):
+        for owner in owners:
+            gap = (owner - z) & (NZ - 1)
+            here = gap != 0
+            if p < 2:
+                here = here & (gap != 2) & (gap != 6)
+
+            @pl.when(here)
+            def _():
+                piece(p, owner, owner, 0).wait_recv()
+
+    def halo():
+        return remote(hx.at[:, 520:528], hx.at[:, 8:16], hs, hr, seq=(me + 1) & (NS - 1))
 
     first(early)
+    for h in range(2):
+        load_h(late, h).wait()
     pl.semaphore_wait(barrier, NS - 1 + NZ - 1)
+
+    @pl.when(me < NS - 1)
+    def _():
+        halo().start()
+
     send_piece(0)
     first(late)
     send_piece(1)
-
-    def halo():
-        return remote(hx.at[:, 520:528], hx.at[:, 8:16], hs, hr, seq=(me + 1) & (NS - 1))
-
-    @pl.when(me < NS - 1)
-    def _():
-        halo().start()
 
     lane = lax.broadcasted_iota(jnp.int32, (LEN, 128), 1)
     is_head = (lane >= HL) & (lane < HL + HEADS)
@@ -204,7 +221,7 @@
             so_far = so_far + total
         off = jnp.concatenate(off, axis=0)
         av[s] = dot(split(size * jnp.exp(-off)), ee[...])
-        ev[s] = dot(split(jnp.exp(off)), ee[...])
+        es[s] = split(jnp.exp(off))
         rows = jnp.concatenate(halves + ahead + [jnp.zeros((8, 128), F32)], axis=0)
         rx[s] = dot(split(rows), ee[...])[0:8, :]
         dsum[pl.ds(s, 1), :] = so_far
@@ -228,7 +245,6 @@
     for peer in others:
         decay(None, peer).start()
     dall[me] = dsum[...]
-    pass_piece(0)
 
     @pl.when(me > 0)
     def _():
@@ -241,7 +257,8 @@
     gap = jnp.zeros((56, 128), F32)
     tail = jnp.concatenate([gap, got[8:16, 0:128], gap, got[0:8, 0:128]], axis=0).T
     bhl[z] = tail[0:32, :].astype(BF16)
-    send_piece(2)
+    for step in far_first:
+        piece(2, z, away(step), step & (NZ - 1)).start()
 
     load_v1.wait()
 
@@ -264,11 +281,12 @@
     project(early, 0)
     project(early, 1)
     for at in range(2):
+        pass_piece(at, to_b)
         project(late, at)
         value(early, 2 * at)
         value(early, 2 * at + 1)
-    pass_piece(1)
-    pass_piece(2)
+    for at in range(2):
+        pass_piece(at, -to_b)
     for b in range(NB):
         value(late, b)
 
@@ -320,11 +338,12 @@
     def across(s, n):
         return remote(st.at[s], so.at[s], cs.at[n], cr.at[n], seq=me + 1 - 2 * core)
 
-    rest_of_piece(2)
-    rest_of_piece(0)
+    b_owners, c_owners = range(4), range(4, 8)
+    rest_of_piece(2, b_owners)
+    rest_of_piece(0, b_owners)
     states(early)
     across(early, 0).start()
-    rest_of_piece(1)
+    rest_of_piece(1, b_owners)
     states(late)
 
     @pl.when(core == 0)
@@ -357,7 +376,10 @@
             right = jnp.concatenate([vv[s, rows, :], sbl[s, b]], axis=0)
             g[s, rows, :] = dot(left, right)
 
+    rest_of_piece(2, c_owners)
+    rest_of_piece(0, c_owners)
     within(early)
+    rest_of_piece(1, c_owners)
     within(late)
 
     for k, own in chips:
@@ -383,7 +405,8 @@
     def gate(s, _):
         for at, wide in ((0, 256), (256, 256), (512, 128)):
             got = dot(hx[s, PAD : PAD + LEN, :], w[:, 768 + at : 768 + at + wide])
-            fg[s, :, at : at + wide] = silu(got) * ev[s, :, at : at + wide]
+            factor = dot(es[s], ee[:, at : at + wide])
+            fg[s, :, at : at + wide] = silu(got) * factor
         return 0
 
     lax.fori_loop(0, 2, gate, 0)
@@ -426,21 +449,23 @@
     def total_sq(owner, peer):
         return remote(ssm, ssa.at[owner], zs.at[peer], zr.at[owner], tp=peer)
 
-    for step in (4, 3, -3, 2, -2, 1, -1):
+    for step in far_first:
         total_sq(z, away(step)).start()
     ssa[z] = ssm[...]
     gains = gn[...].reshape(1, CI)
     for s in range(2):
         out[s] = g[s] * gains
-    for step in (4, 3, -3, 2, -2, 1, -1):
+    for step in far_first:
         total_sq(away(step), away(step)).wait_recv()
     rms[...] = lax.rsqrt(jnp.sum(ssa[...], axis=0) * (1.0 / DI) + EPS)
 
-    for p in range(3):
+    for p in range(2):
         for step, n in near:
             piece(p, z, away(step), n).wait_send()
-        for owner, target, n in passed_on(p):
-            piece(p, away(owner), away(target), n).wait_send()
+        for way in (1, -1):
+            passed_on(p, way, lambda copy: copy.wait_send())
+    for step in far_first:
+        piece(2, z, away(step), step & (NZ - 1)).wait_send()
     for step in range(1, NZ):
         total_sq(z, away(step)).wait_send()
 
@@ -501,7 +526,7 @@
         vmem((2, LEN, 128), BF16),
         vmem((2, 128, LEN), BF16),
         vmem((2, LEN, CI), F32),
-        vmem((2, LEN, CI), F32),
+        vmem((2, LEN, 256), BF16),
         vmem((2, LEN, CI), F32),
         vmem((2, LEN, CI), F32),
         vmem((2, 8, CI), F32),
@@ -523,7 +548,7 @@
         dma((14,)),
         dma,
         dma,
-        dma((3, 7)),
+        dma((3, NZ)),
         dma((3, NZ)),
         dma((NS,)),
         dma((NS,)),

time: 45.5 us -> 42.7 us (0.938)
  Pallas kernels: 45.3 us -> 42.4 us
    pallas_call x1, Pallas kernels: 44 us -> 41.2 us  [on_device(): pl.pallas_call(kernel, out_shape=(vmem((2, LEN, CI), F32), vmem((8, 128),...]
where the time goes in v5:
time: 42.7 us; the launch traced here: 42.6 us
  Pallas kernels  42.4 us (99%)
    pallas_call x1, Pallas kernels, on_device(): pl.pallas_call(kernel, out_shape=(vmem((2, LEN, CI), F32), vmem((8, 128),...  41.2 us
    pallas_call x1, Pallas kernels, on_device(): pl.pallas_call(scaled, out_shape=jax.ShapeDtypeStruct((2, LEN, CI), BF16)...  1.22 us

profile of v5, /device:TPU:1, one launch (start us, length us, event | category | flops | bytes accessed | tf_op | source)
XLA Modules:
  0.0 42.6 jit_solution(10787826820923158887)
XLA Ops:
  0.0 41.2 %shard_map.100 = (f32[2,512,640]{2,1,0:T(8,128)S(1)}, f32[8,128]{1,0:T(8,128)S(1)}) custom-call(bf16[2,512,2560]{2,1,0:T(8,128)(2,1)} %hid.1, bf16[2560,640]{1,0:T(8,128)(2,1)} %gw.1, bf16[2560,640]{1,0:T(8,128)(2,1)} %vw.1, bf16[32,2560]{1,0:T(8,128)(2,1)} %bitcast.4, bf16[10,2560]{1,0:T(8,128)(2,1)} %bitcast.5, f32[4,640]{1,0:T(4,128)} %vconv.1, ...), custom_call_target="tpu_custom_call" | custom-call | tf_op jit(solution)/shard_map/pallas_call | solution.py:565
  41.2 1.2 %shard_map.101 = bf16[2,512,640]{2,1,0:T(8,128)(2,1)} custom-call(f32[2,512,640]{2,1,0:T(8,128)S(1)} %get-tuple-element.7.gated, f32[8,128]{1,0:T(8,128)S(1)} %get-tuple-element.8.rms), custom_call_target="tpu_custom_call" | custom-call | tf_op jit(solution)/shard_map/pallas_call | solution.py:578

commit v6 on v5

--- a/solution.py
+++ b/solution.py
@@ -39,7 +39,7 @@
     hid, gw, vw, bw, sw, vconv, bconv, sbias, lrate, gain, out, rms,
     hx, w, bwv, swv, cv, bcv, sb, lr, gn, prm, tap, ee, bs, vp, bct, cmat, bmat,
     av, es, fg, g, rx, dsum, dall, dxl, dx, bhl, vv, sbl, st, so, agg, p1, po, pin, ssm, ssa,
-    ld, hs, hr, bsend, brecv, dsend, drecv, s1, r1, s2, r2, zs, zr, cs, cr,
+    ld, hs, hr, bsend, brecv, bhs, bhr, dsend, drecv, s1, r1, s2, r2, zs, zr, cs, cr,
 ):
     me, z = lax.axis_index("seq"), lax.axis_index("tp")
     core, chip = me & 1, lax.div(me, 2)
@@ -50,6 +50,22 @@
         return pltpu.make_async_remote_copy(
             src_ref=src, dst_ref=dst, send_sem=ss, recv_sem=rs, device_id=where, device_id_type=MESH
         )
+
+    barrier = pltpu.get_barrier_semaphore()
+
+    def greet_seq(r, _):
+        pl.semaphore_signal(
+            barrier, inc=1, device_id={"seq": (me + r) & (NS - 1), "tp": z}, device_id_type=MESH
+        )
+        return 0
+
+    def greet_tp(r, _):
+        pl.semaphore_signal(
+            barrier, inc=1, device_id={"seq": me, "tp": (z + r) & (NZ - 1)}, device_id_type=MESH
+        )
+        return 0
+
+    lax.fori_loop(1, NZ, greet_tp, 0)
 
     small = [
         pltpu.make_async_copy(src, dst, ld.at[9 + n])
@@ -73,28 +89,10 @@
     for copy in small:
         copy.start()
     load_v0.start()
-    for s in (early, late):
-        for h in range(2):
-            load_h(s, h).start()
-    load_v1.start()
-    load_g.start()
-
-    barrier = pltpu.get_barrier_semaphore()
-
-    def greet_seq(r, _):
-        pl.semaphore_signal(
-            barrier, inc=1, device_id={"seq": (me + r) & (NS - 1), "tp": z}, device_id_type=MESH
-        )
-        return 0
-
-    def greet_tp(r, _):
-        pl.semaphore_signal(
-            barrier, inc=1, device_id={"seq": me, "tp": (z + r) & (NZ - 1)}, device_id_type=MESH
-        )
-        return 0
+    for h in range(2):
+        load_h(early, h).start()
 
     lax.fori_loop(1, NS, greet_seq, 0)
-    lax.fori_loop(1, NZ, greet_tp, 0)
 
     row = lax.broadcasted_iota(jnp.int32, (256, CI), 0)
     col = lax.broadcasted_iota(jnp.int32, (256, CI), 1)
@@ -129,6 +127,8 @@
             [bwv[:, lanes].astype(F32), swv[:, lanes].astype(F32), jnp.zeros((86, 128), F32)], axis=0
         )
         w[lanes, 0:128] = both.T.astype(BF16)
+    for h in range(2):
+        load_h(late, h).start()
     load_v0.wait()
 
     def first(s):
@@ -143,61 +143,77 @@
             turned = bs[s, Q * b : Q * b + Q, :].T
             bct[s, z, :, Q * b : Q * b + Q] = turned[0:32, :].astype(BF16)
 
-    def piece(p, owner, peer, n):
-        part = bct.at[(early, late)[p], owner] if p < 2 else bhl.at[owner]
-        return remote(part, part, bsend.at[p, n], brecv.at[p, owner], tp=peer)
+    def piece(p, owner, peer):
+        if p == 2:
+            return remote(bhl.at[owner], bhl.at[owner], bhs, bhr, tp=peer)
+        part = bct.at[(early, late)[p], owner]
+        return remote(part, part, bsend, brecv.at[p, owner], tp=peer)
 
     def away(n):
         return (z + n) & (NZ - 1)
 
-    near = ((2, 0), (-2, 1), (1, 2), (-1, 3))
+    near = (2, -2, 1, -1)
     far_first = (4, 3, -3, 2, -2, 1, -1)
     to_b = jnp.where((z >= 2) & (z < 6), 1, -1)
 
-    def send_piece(p):
-        for step, n in near:
-            piece(p, z, away(step), n).start()
-
-    def passed_on(p, way, act):
+    def send_piece(p, steps):
+        for step in near[steps]:
+            piece(p, z, away(step)).start()
+
+    def pass_piece(p, way):
         owner = away(-2 * way)
-        n = jnp.where(way > 0, 4, 5)
-        act(piece(p, owner, away(way), n))
+        piece(p, owner, owner).wait_recv()
+        piece(p, owner, away(way)).start()
 
         @pl.when(way == (-1 if p else 1))
         def _():
-            act(piece(p, owner, away(2 * way), 6))
-
-    def pass_piece(p, way):
-        owner = away(-2 * way)
-        piece(p, owner, owner, 0).wait_recv()
-        passed_on(p, way, lambda copy: copy.start())
+            piece(p, owner, away(2 * way)).start()
 
     def rest_of_piece(p, owners):
         for owner in owners:
             gap = (owner - z) & (NZ - 1)
-            here = gap != 0
-            if p < 2:
-                here = here & (gap != 2) & (gap != 6)
-
-            @pl.when(here)
+
+            @pl.when((gap != 0) & (gap != 2) & (gap != 6))
             def _():
-                piece(p, owner, owner, 0).wait_recv()
+                piece(p, owner, owner).wait_recv()
+
+    def all_of(part, ss, rs):
+        return remote(part, part, ss, rs, tp=away(1))
 
     def halo():
         return remote(hx.at[:, 520:528], hx.at[:, 8:16], hs, hr, seq=(me + 1) & (NS - 1))
 
+    ahead = z < NZ // 2
     first(early)
+    load_v1.start()
     for h in range(2):
         load_h(late, h).wait()
+
+    @pl.when(ahead)
+    def _():
+        first(late)
+
     pl.semaphore_wait(barrier, NS - 1 + NZ - 1)
 
     @pl.when(me < NS - 1)
     def _():
         halo().start()
 
-    send_piece(0)
-    first(late)
-    send_piece(1)
+    send_piece(0, slice(0, 2))
+
+    @pl.when(jnp.logical_not(ahead))
+    def _():
+        send_piece(0, slice(2, 4))
+        first(late)
+
+    load_g.start()
+    send_piece(1, slice(0, 2))
+
+    @pl.when(ahead)
+    def _():
+        send_piece(0, slice(2, 4))
+
+    send_piece(1, slice(2, 4))
 
     lane = lax.broadcasted_iota(jnp.int32, (LEN, 128), 1)
     is_head = (lane >= HL) & (lane < HL + HEADS)
@@ -237,13 +253,11 @@
     chips = [(((y + dy) & 3) * 4 + ((x + dx) & 3), (dy, dx) == (0, 0)) for dy, dx in offsets]
     others = [2 * c + n for c, own in chips for n in range(2) if not own] + [me + 1 - 2 * core]
 
-    def decay(owner, peer):
-        src = dsum if owner is None else dall.at[owner]
-        slot = me if owner is None else owner
-        return remote(src, dall.at[slot], dsend.at[peer], drecv.at[slot], seq=peer)
+    def decay(peer):
+        return remote(dsum, dall.at[me], dsend, drecv, seq=peer)
 
     for peer in others:
-        decay(None, peer).start()
+        decay(peer).start()
     dall[me] = dsum[...]
 
     @pl.when(me > 0)
@@ -258,7 +272,7 @@
     tail = jnp.concatenate([gap, got[8:16, 0:128], gap, got[0:8, 0:128]], axis=0).T
     bhl[z] = tail[0:32, :].astype(BF16)
     for step in far_first:
-        piece(2, z, away(step), step & (NZ - 1)).start()
+        piece(2, z, away(step)).start()
 
     load_v1.wait()
 
@@ -280,15 +294,23 @@
 
     project(early, 0)
     project(early, 1)
+    pass_piece(0, to_b)
+
+    @pl.when(ahead)
+    def _():
+        pass_piece(1, to_b)
+
     for at in range(2):
-        pass_piece(at, to_b)
         project(late, at)
         value(early, 2 * at)
         value(early, 2 * at + 1)
+
+    @pl.when(jnp.logical_not(ahead))
+    def _():
+        pass_piece(1, to_b)
+
     for at in range(2):
         pass_piece(at, -to_b)
-    for b in range(NB):
-        value(late, b)
 
     def mix(s, h):
         ahead = bhl[4 * h : 4 * h + 4].astype(F32).reshape(128, 128)
@@ -305,8 +327,7 @@
             blocks.append(silu(mixed))
         return blocks
 
-    for peer in others:
-        decay(peer, peer).wait_recv()
+    all_of(dall.at[0 : NS - 1], dsend, drecv).wait_recv()
 
     def pick(j, _):
         dxl[pl.ds(j, 1), :] = dall[2 * j, pl.ds(core, 1), :] + dall[2 * j + 1, pl.ds(core, 1), :]
@@ -339,10 +360,12 @@
         return remote(st.at[s], so.at[s], cs.at[n], cr.at[n], seq=me + 1 - 2 * core)
 
     b_owners, c_owners = range(4), range(4, 8)
-    rest_of_piece(2, b_owners)
+    all_of(bhl.at[0 : NZ - 1], bhs, bhr).wait_recv()
     rest_of_piece(0, b_owners)
     states(early)
     across(early, 0).start()
+    for b in range(NB):
+        value(late, b)
     rest_of_piece(1, b_owners)
     states(late)
 
@@ -351,7 +374,7 @@
         across(0, 1).start()
 
     def first_hop(source, k):
-        return remote(agg.at[k], p1.at[source], s1.at[k], r1.at[source], seq=2 * k + core)
+        return remote(agg.at[k], p1.at[source], s1, r1, seq=2 * k + core)
 
     across(late, 0).wait_recv()
     carry = dx[16:17, :]
@@ -363,6 +386,22 @@
             p1[k] = agg[k]
         else:
             first_hop(chip, k).start()
+
+    load_g.wait()
+
+    def gate(s):
+        for top, rows, at, wide in (
+            (0, LEN, 0, 256),
+            (0, LEN, 256, 256),
+            (0, LEN // 2, 512, 128),
+            (LEN // 2, LEN // 2, 512, 128),
+        ):
+            here = slice(top, top + rows)
+            got = dot(hx[s, PAD + top : PAD + top + rows, :], w[:, 768 + at : 768 + at + wide])
+            factor = dot(es[s, here, :], ee[:, at : at + wide])
+            fg[s, here, at : at + wide] = silu(got) * factor
+
+    gate(early)
 
     def within(s):
         for b, block in enumerate(mix(s, 1)):
@@ -376,15 +415,12 @@
             right = jnp.concatenate([vv[s, rows, :], sbl[s, b]], axis=0)
             g[s, rows, :] = dot(left, right)
 
-    rest_of_piece(2, c_owners)
     rest_of_piece(0, c_owners)
     within(early)
     rest_of_piece(1, c_owners)
     within(late)
 
-    for k, own in chips:
-        if not own:
-            first_hop(k, chip).wait_recv()
+    all_of(p1.at[0:15], s1, r1).wait_recv()
     so_far = jnp.zeros((8, CI), F32)
     for j in range(16):
         po[j] = so_far.astype(BF16)
@@ -392,7 +428,7 @@
 
     def second_hop(target, source):
         slot = pin.at[late, source]
-        return remote(po.at[target], slot, s2.at[target], r2.at[source], seq=2 * target + core)
+        return remote(po.at[target], slot, s2, r2, seq=2 * target + core)
 
     for k, own in chips:
         if own:
@@ -400,23 +436,12 @@
         else:
             second_hop(k, chip).start()
 
-    load_g.wait()
-
-    def gate(s, _):
-        for at, wide in ((0, 256), (256, 256), (512, 128)):
-            got = dot(hx[s, PAD : PAD + LEN, :], w[:, 768 + at : 768 + at + wide])
-            factor = dot(es[s], ee[:, at : at + wide])
-            fg[s, :, at : at + wide] = silu(got) * factor
-        return 0
-
-    lax.fori_loop(0, 2, gate, 0)
+    gate(late)
 
     ones = jnp.ones((16, 128), BF16)
     at_row = lax.broadcasted_iota(jnp.int32, (8, 128), 0)
     squares = jnp.zeros((8, 128), F32)
-    for k, own in chips:
-        if not own:
-            second_hop(k, k).wait_recv()
+    all_of(po.at[0:15], s2, r2).wait_recv()
 
     def back(s):
         return remote(pin.at[s], pin.at[s], cs.at[2], cr.at[2], seq=me + 1 - 2 * core)
@@ -447,34 +472,20 @@
     ssm[...] = squares
 
     def total_sq(owner, peer):
-        return remote(ssm, ssa.at[owner], zs.at[peer], zr.at[owner], tp=peer)
+        return remote(ssm, ssa.at[owner], zs, zr, tp=peer)
 
     for step in far_first:
         total_sq(z, away(step)).start()
     ssa[z] = ssm[...]
     gains = gn[...].reshape(1, CI)
     for s in range(2):
-        out[s] = g[s] * gains
-    for step in far_first:
-        total_sq(away(step), away(step)).wait_recv()
-    rms[...] = lax.rsqrt(jnp.sum(ssa[...], axis=0) * (1.0 / DI) + EPS)
-
-    for p in range(2):
-        for step, n in near:
-            piece(p, z, away(step), n).wait_send()
-        for way in (1, -1):
-            passed_on(p, way, lambda copy: copy.wait_send())
-    for step in far_first:
-        piece(2, z, away(step), step & (NZ - 1)).wait_send()
-    for step in range(1, NZ):
-        total_sq(z, away(step)).wait_send()
-
-    for peer in others:
-        decay(None, peer).wait_send()
-    for k, own in chips:
-        if not own:
-            first_hop(chip, k).wait_send()
-            second_hop(k, chip).wait_send()
+        out[s] = (g[s] * gains).astype(BF16)
+
+    all_of(bct.at[:, 0 : NZ - 1], bsend, bsend).wait_send()
+    all_of(bhl.at[0 : NZ - 1], bhs, bhr).wait_send()
+    all_of(dall.at[0 : NS - 1], dsend, drecv).wait_send()
+    all_of(p1.at[0:15], s1, r1).wait_send()
+    all_of(po.at[0:15], s2, r2).wait_send()
     across(early, 0).wait_send()
     back(late).wait_send()
 
@@ -485,6 +496,10 @@
     @pl.when(me < NS - 1)
     def _():
         halo().wait_send()
+
+    all_of(ssa.at[0 : NZ - 1], zs, zr).wait_recv()
+    rms[...] = lax.rsqrt(jnp.sum(ssa[...], axis=0) * (1.0 / DI) + EPS)
+    all_of(ssa.at[0 : NZ - 1], zs, zr).wait_send()
 
 
 def scaled(gated, rms, out, osc, sems):
@@ -496,7 +511,7 @@
             by_token = jnp.broadcast_to(rms[n : n + 1, :], (128, 128)).T
             for c in range(5):
                 lanes = slice(128 * c, 128 * c + 128)
-                osc[s, rows, lanes] = (gated[s, rows, lanes] * by_token).astype(BF16)
+                osc[s, rows, lanes] = (gated[s, rows, lanes].astype(F32) * by_token).astype(BF16)
             copies.append(pltpu.make_async_copy(osc.at[s, rows], out.at[s, rows], sems.at[n]))
             copies[-1].start()
     for copy in copies:
@@ -548,23 +563,25 @@
         dma((14,)),
         dma,
         dma,
-        dma((3, NZ)),
-        dma((3, NZ)),
-        dma((NS,)),
-        dma((NS,)),
-        dma((16,)),
-        dma((16,)),
-        dma((16,)),
-        dma((16,)),
-        dma((NZ,)),
-        dma((NZ,)),
+        dma,
+        dma((2, NZ)),
+        dma,
+        dma,
+        dma,
+        dma,
+        dma,
+        dma,
+        dma,
+        dma,
+        dma,
+        dma,
         dma((3,)),
         dma((3,)),
     ]
     in_vmem = pl.BlockSpec(memory_space=vmem)
     gated, rms = pl.pallas_call(
         kernel,
-        out_shape=(vmem((2, LEN, CI), F32), vmem((8, 128), F32)),
+        out_shape=(vmem((2, LEN, CI), BF16), vmem((8, 128), F32)),
         in_specs=[any_space] * 10,
         out_specs=(in_vmem, in_vmem),
         scratch_shapes=scratch,

time: 42.7 us -> 40.9 us (0.958)
  Pallas kernels: 42.4 us -> 40.6 us
    pallas_call x1, Pallas kernels: 41.2 us -> 39.4 us  [on_device(): pl.pallas_call(kernel, out_shape=(vmem((2, LEN, CI), BF16), vmem((8, 128)...]
where the time goes in v6:
time: 40.9 us; the launch traced here: 40.8 us
  Pallas kernels  40.6 us (99%)
    pallas_call x1, Pallas kernels, on_device(): pl.pallas_call(kernel, out_shape=(vmem((2, LEN, CI), BF16), vmem((8, 128)...  39.4 us
    pallas_call x1, Pallas kernels, on_device(): pl.pallas_call(scaled, out_shape=jax.ShapeDtypeStruct((2, LEN, CI), BF16)...  1.24 us

profile of v6, /device:TPU:1, one launch (start us, length us, event | category | flops | bytes accessed | tf_op | source)
XLA Modules:
  0.0 40.8 jit_solution(13290703956332094649)
XLA Ops:
  0.0 39.4 %shard_map.100 = (bf16[2,512,640]{2,1,0:T(8,128)(2,1)S(1)}, f32[8,128]{1,0:T(8,128)S(1)}) custom-call(bf16[2,512,2560]{2,1,0:T(8,128)(2,1)} %hid.1, bf16[2560,640]{1,0:T(8,128)(2,1)} %gw.1, bf16[2560,640]{1,0:T(8,128)(2,1)} %vw.1, bf16[32,2560]{1,0:T(8,128)(2,1)} %bitcast.4, bf16[10,2560]{1,0:T(8,128)(2,1)} %bitcast.5, f32[4,640]{1,0:T(4,128)} %vconv.1, ...), custom_call_target="tpu_custom_call" | custom-call | tf_op jit(solution)/shard_map/pallas_call | solution.py:582
  39.4 1.2 %shard_map.101 = bf16[2,512,640]{2,1,0:T(8,128)(2,1)} custom-call(bf16[2,512,640]{2,1,0:T(8,128)(2,1)S(1)} %get-tuple-element.7.gated, f32[8,128]{1,0:T(8,128)S(1)} %get-tuple-element.8.rms), custom_call_target="tpu_custom_call" | custom-call | tf_op jit(solution)/shard_map/pallas_call | solution.py:595

commit v7 on v6

--- a/solution.py
+++ b/solution.py
@@ -132,13 +132,13 @@
     load_v0.wait()
 
     def first(s):
-        for h in range(2):
-            if s is early:
-                load_h(s, h).wait()
-            at = 256 * h
-            got = dot(hx[s, PAD + at : PAD + at + 256, :], w[:, 0:256])
-            bs[s, at : at + 256, :] = got[:, 0:128]
-            vp[s, 0, PAD + at : PAD + at + 256, :] = got[:, 128:256]
+        rows = 128 if s is early else 256
+        for at in range(0, LEN, rows):
+            if s is early and at % 256 == 0:
+                load_h(s, at // 256).wait()
+            got = dot(hx[s, PAD + at : PAD + at + rows, :], w[:, 0:256])
+            bs[s, at : at + rows, :] = got[:, 0:128]
+            vp[s, 0, PAD + at : PAD + at + rows, :] = got[:, 128:256]
         for b in range(NB):
             turned = bs[s, Q * b : Q * b + Q, :].T
             bct[s, z, :, Q * b : Q * b + Q] = turned[0:32, :].astype(BF16)
@@ -156,6 +156,8 @@
     far_first = (4, 3, -3, 2, -2, 1, -1)
     to_b = jnp.where((z >= 2) & (z < 6), 1, -1)
 
+    ahead = z < NZ // 2
+
     def send_piece(p, steps):
         for step in near[steps]:
             piece(p, z, away(step)).start()
@@ -165,7 +167,7 @@
         piece(p, owner, owner).wait_recv()
         piece(p, owner, away(way)).start()
 
-        @pl.when(way == (-1 if p else 1))
+        @pl.when(way == jnp.where(ahead, to_b, -to_b))
         def _():
             piece(p, owner, away(2 * way)).start()
 
@@ -183,7 +185,6 @@
     def halo():
         return remote(hx.at[:, 520:528], hx.at[:, 8:16], hs, hr, seq=(me + 1) & (NS - 1))
 
-    ahead = z < NZ // 2
     first(early)
     load_v1.start()
     for h in range(2):
@@ -207,13 +208,12 @@
         first(late)
 
     load_g.start()
-    send_piece(1, slice(0, 2))
 
     @pl.when(ahead)
     def _():
+        send_piece(1, slice(0, 2))
         send_piece(0, slice(2, 4))
-
-    send_piece(1, slice(2, 4))
+        send_piece(1, slice(2, 4))
 
     lane = lax.broadcasted_iota(jnp.int32, (LEN, 128), 1)
     is_head = (lane >= HL) & (lane < HL + HEADS)
@@ -265,12 +265,12 @@
         halo().wait_recv()
 
     both = jnp.concatenate([hx[0, 8:16, :], hx[1, 8:16, :]], axis=0)
-    got = dot(both, w[:, 0:256])
+    got = dot(both[:, : D // 2], w[: D // 2, 0:256]) + dot(both[:, D // 2 :], w[D // 2 :, 0:256])
     for s in range(2):
         vp[s, 0, 8:16, :] = got[8 * s : 8 * s + 8, 128:256]
-    gap = jnp.zeros((56, 128), F32)
-    tail = jnp.concatenate([gap, got[8:16, 0:128], gap, got[0:8, 0:128]], axis=0).T
-    bhl[z] = tail[0:32, :].astype(BF16)
+    tail = jnp.concatenate([got[12:16, 0:128], got[4:8, 0:128]], axis=0)
+    tail = jnp.where(lax.broadcasted_iota(jnp.int32, (8, 128), 1) < 32, tail, 0.0)
+    bhl[z] = pltpu.roll(tail, 32 * (z & 3), 1).astype(BF16)
     for step in far_first:
         piece(2, z, away(step)).start()
 
@@ -292,31 +292,36 @@
             here = (s, slice(Q * b, Q * b + Q), lanes)
             vv[here] = (silu(mixed) * av[here]).astype(BF16)
 
+
+    @pl.when(jnp.logical_not(ahead))
+    def _():
+        pass_piece(0, to_b)
+
     project(early, 0)
     project(early, 1)
-    pass_piece(0, to_b)
 
     @pl.when(ahead)
     def _():
-        pass_piece(1, to_b)
-
-    for at in range(2):
-        project(late, at)
-        value(early, 2 * at)
-        value(early, 2 * at + 1)
+        pass_piece(0, to_b)
+
+    pass_piece(1, to_b)
 
     @pl.when(jnp.logical_not(ahead))
     def _():
-        pass_piece(1, to_b)
-
-    for at in range(2):
-        pass_piece(at, -to_b)
+        send_piece(1, slice(0, 4))
+
+    project(late, 0)
+    project(late, 1)
+    for b in range(NB):
+        value(early, b)
+    pass_piece(0, -to_b)
 
     def mix(s, h):
-        ahead = bhl[4 * h : 4 * h + 4].astype(F32).reshape(128, 128)
-        ahead = jnp.where(s == 1, pltpu.roll(ahead, 64, 1), ahead)
+        rows = jnp.sum(bhl[4 * h : 4 * h + 4].astype(F32), axis=0)
+        rows = jnp.where(s == 1, rows[0:4], rows[4:8])
+        before = jnp.concatenate([jnp.zeros((124, 128), F32), rows], axis=0).T
         x = bct[s, 4 * h : 4 * h + 4].astype(F32).reshape(128, LEN)
-        x = jnp.concatenate([ahead, x], axis=1)
+        x = jnp.concatenate([before, x], axis=1)
         turned = [pltpu.roll(x, 3 - k, 1) for k in range(3)] + [x]
         blocks = []
         for b in range(NB):
@@ -387,6 +392,8 @@
         else:
             first_hop(chip, k).start()
 
+    pass_piece(1, -to_b)
+
     load_g.wait()
 
     def gate(s):
@@ -417,8 +424,6 @@
 
     rest_of_piece(0, c_owners)
     within(early)
-    rest_of_piece(1, c_owners)
-    within(late)
 
     all_of(p1.at[0:15], s1, r1).wait_recv()
     so_far = jnp.zeros((8, CI), F32)
@@ -436,6 +441,8 @@
         else:
             second_hop(k, chip).start()
 
+    rest_of_piece(1, c_owners)
+    within(late)
     gate(late)
 
     ones = jnp.ones((16, 128), BF16)
@@ -549,7 +556,7 @@
         vmem((NS, 8, 128), F32),
         vmem((NS, 128), F32),
         vmem((NS, CI), F32),
-        vmem((NZ, 32, 128), BF16),
+        vmem((NZ, 8, 128), BF16),
         vmem((2, LEN, CI), BF16),
         vmem((2, NB, 128, CI), BF16),
         vmem((2, 16, 8, CI), BF16),

time: 40.9 us -> 39.7 us (0.971)
  Pallas kernels: 40.6 us -> 39.6 us
    pallas_call x1, Pallas kernels: 39.4 us -> 38.4 us  [on_device(): pl.pallas_call(kernel, out_shape=(vmem((2, LEN, CI), BF16), vmem((8, 128)...]
where the time goes in v7:
time: 39.7 us; the launch traced here: 39.6 us
  Pallas kernels  39.6 us (100%)
    pallas_call x1, Pallas kernels, on_device(): pl.pallas_call(kernel, out_shape=(vmem((2, LEN, CI), BF16), vmem((8, 128)...  38.4 us
    pallas_call x1, Pallas kernels, on_device(): pl.pallas_call(scaled, out_shape=jax.ShapeDtypeStruct((2, LEN, CI), BF16)...  1.24 us

profile of v7, /device:TPU:1, one launch (start us, length us, event | category | flops | bytes accessed | tf_op | source)
XLA Modules:
  0.0 39.6 jit_solution(6207154809481394421)
XLA Ops:
  0.0 38.4 %shard_map.100 = (bf16[2,512,640]{2,1,0:T(8,128)(2,1)S(1)}, f32[8,128]{1,0:T(8,128)S(1)}) custom-call(bf16[2,512,2560]{2,1,0:T(8,128)(2,1)} %hid.1, bf16[2560,640]{1,0:T(8,128)(2,1)} %gw.1, bf16[2560,640]{1,0:T(8,128)(2,1)} %vw.1, bf16[32,2560]{1,0:T(8,128)(2,1)} %bitcast.4, bf16[10,2560]{1,0:T(8,128)(2,1)} %bitcast.5, f32[4,640]{1,0:T(4,128)} %vconv.1, ...), custom_call_target="tpu_custom_call" | custom-call | tf_op jit(solution)/shard_map/pallas_call | solution.py:589
  38.4 1.2 %shard_map.101 = bf16[2,512,640]{2,1,0:T(8,128)(2,1)} custom-call(bf16[2,512,640]{2,1,0:T(8,128)(2,1)S(1)} %get-tuple-element.7.gated, f32[8,128]{1,0:T(8,128)S(1)} %get-tuple-element.8.rms), custom_call_target="tpu_custom_call" | custom-call | tf_op jit(solution)/shard_map/pallas_call | solution.py:602

commit v8 on v7

--- a/solution.py
+++ b/solution.py
@@ -68,7 +68,7 @@
     lax.fori_loop(1, NZ, greet_tp, 0)
 
     small = [
-        pltpu.make_async_copy(src, dst, ld.at[9 + n])
+        pltpu.make_async_copy(src, dst, ld.at[8 + n])
         for n, (src, dst) in enumerate(
             [(vconv, cv), (bconv, bcv), (sbias, sb), (lrate, lr), (gain, gn)]
         )
@@ -76,12 +76,12 @@
     load_b = pltpu.make_async_copy(bw, bwv, ld.at[0])
     load_s = pltpu.make_async_copy(sw, swv, ld.at[1])
     load_v0 = pltpu.make_async_copy(vw.at[:, 0:128], w.at[:, 128:256], ld.at[2])
-    load_v1 = pltpu.make_async_copy(vw.at[:, 128:CI], w.at[:, 256:768], ld.at[7])
-    load_g = pltpu.make_async_copy(gw, w.at[:, 768:1408], ld.at[8])
+    load_v1 = pltpu.make_async_copy(vw.at[:, 128:CI], w.at[:, 256:768], ld.at[6])
+    load_g = pltpu.make_async_copy(gw, w.at[:, 768:1408], ld.at[7])
 
     def load_h(s, h):
         return pltpu.make_async_copy(
-            hid.at[s, pl.ds(256 * h, 256)], hx.at[s, pl.ds(PAD + 256 * h, 256)], ld.at[3 + 2 * s + h]
+            hid.at[s, pl.ds(256 * h, 256)], hx.at[s, pl.ds(PAD + 256 * h, 256)], ld.at[3 + h]
         )
 
     load_b.start()
@@ -127,8 +127,8 @@
             [bwv[:, lanes].astype(F32), swv[:, lanes].astype(F32), jnp.zeros((86, 128), F32)], axis=0
         )
         w[lanes, 0:128] = both.T.astype(BF16)
-    for h in range(2):
-        load_h(late, h).start()
+    load_late = pltpu.make_async_copy(hid.at[late], hx.at[late, PAD : PAD + LEN], ld.at[5])
+    load_late.start()
     load_v0.wait()
 
     def first(s):
@@ -187,8 +187,7 @@
 
     first(early)
     load_v1.start()
-    for h in range(2):
-        load_h(late, h).wait()
+    load_late.wait()
 
     @pl.when(ahead)
     def _():
@@ -211,9 +210,8 @@
 
     @pl.when(ahead)
     def _():
-        send_piece(1, slice(0, 2))
         send_piece(0, slice(2, 4))
-        send_piece(1, slice(2, 4))
+        send_piece(1, slice(0, 4))
 
     lane = lax.broadcasted_iota(jnp.int32, (LEN, 128), 1)
     is_head = (lane >= HL) & (lane < HL + HEADS)
@@ -519,8 +517,10 @@
             for c in range(5):
                 lanes = slice(128 * c, 128 * c + 128)
                 osc[s, rows, lanes] = (gated[s, rows, lanes].astype(F32) * by_token).astype(BF16)
-            copies.append(pltpu.make_async_copy(osc.at[s, rows], out.at[s, rows], sems.at[n]))
-            copies[-1].start()
+            if b % 2:
+                pair = slice(Q * b - Q, Q * b + Q)
+                copies.append(pltpu.make_async_copy(osc.at[s, pair], out.at[s, pair], sems.at[n // 2]))
+                copies[-1].start()
     for copy in copies:
         copy.wait()
 
@@ -567,7 +567,7 @@
         vmem((2, 16, 8, CI), BF16),
         vmem((8, 128), F32),
         vmem((NZ, 8, 128), F32),
-        dma((14,)),
+        dma((13,)),
         dma,
         dma,
         dma,
@@ -604,7 +604,7 @@
         out_shape=jax.ShapeDtypeStruct((2, LEN, CI), BF16),
         in_specs=[in_vmem, in_vmem],
         out_specs=any_space,
-        scratch_shapes=[vmem((2, LEN, CI), BF16), dma((2 * NB,))],
+        scratch_shapes=[vmem((2, LEN, CI), BF16), dma((NB,))],
     )(*(pltpu.with_memory_space_constraint(x, vmem) for x in (gated, rms)))
 
 

time: 39.7 us -> 39.7 us (level)
  no operation moved by 1% of the time
where the time goes in v8:
time: 39.7 us
  Pallas kernels  39.6 us (100%)
    pallas_call x1, Pallas kernels, on_device(): pl.pallas_call(kernel, out_shape=(vmem((2, LEN, CI), BF16), vmem((8, 128)...  38.4 us
    pallas_call x1, Pallas kernels, on_device(): pl.pallas_call(scaled, out_shape=jax.ShapeDtypeStruct((2, LEN, CI), BF16)...  1.22 us

profile of v8, /device:TPU:1, one launch (start us, length us, event | category | flops | bytes accessed | tf_op | source)
XLA Modules:
  0.0 39.7 jit_solution(14967571346218682756)
XLA Ops:
  0.0 38.4 %shard_map.100 = (bf16[2,512,640]{2,1,0:T(8,128)(2,1)S(1)}, f32[8,128]{1,0:T(8,128)S(1)}) custom-call(bf16[2,512,2560]{2,1,0:T(8,128)(2,1)} %hid.1, bf16[2560,640]{1,0:T(8,128)(2,1)} %gw.1, bf16[2560,640]{1,0:T(8,128)(2,1)} %vw.1, bf16[32,2560]{1,0:T(8,128)(2,1)} %bitcast.4, bf16[10,2560]{1,0:T(8,128)(2,1)} %bitcast.5, f32[4,640]{1,0:T(4,128)} %vconv.1, ...), custom_call_target="tpu_custom_call" | custom-call | tf_op jit(solution)/shard_map/pallas_call | solution.py:589
  38.4 1.2 %shard_map.101 = bf16[2,512,640]{2,1,0:T(8,128)(2,1)} custom-call(bf16[2,512,640]{2,1,0:T(8,128)(2,1)S(1)} %get-tuple-element.7.gated, f32[8,128]{1,0:T(8,128)S(1)} %get-tuple-element.8.rms), custom_call_target="tpu_custom_call" | custom-call | tf_op jit(solution)/shard_map/pallas_call | solution.py:602

commit v9 on v7

--- a/solution.py
+++ b/solution.py
@@ -431,15 +431,15 @@
         po[j] = so_far.astype(BF16)
         so_far = so_far * dx[j : j + 1, :] + p1[j].astype(F32)
 
-    def second_hop(target, source):
+    def second_hop(target, source, group):
         slot = pin.at[late, source]
-        return remote(po.at[target], slot, s2, r2, seq=2 * target + core)
-
-    for k, own in chips:
+        return remote(po.at[target], slot, s2, r2.at[group], seq=2 * target + core)
+
+    for n, (k, own) in enumerate(chips):
         if own:
             pin[late, k] = po[k]
         else:
-            second_hop(k, chip).start()
+            second_hop(k, chip, int(n < 5)).start()
 
     rest_of_piece(1, c_owners)
     within(late)
@@ -448,12 +448,20 @@
     ones = jnp.ones((16, 128), BF16)
     at_row = lax.broadcasted_iota(jnp.int32, (8, 128), 0)
     squares = jnp.zeros((8, 128), F32)
-    all_of(po.at[0:15], s2, r2).wait_recv()
 
     def back(s):
         return remote(pin.at[s], pin.at[s], cs.at[2], cr.at[2], seq=me + 1 - 2 * core)
 
-    back(late).start()
+    def back_slab(k):
+        slab = pin.at[late, k]
+        return remote(slab, slab, cs.at[2], cr.at[2], seq=me + 1 - 2 * core)
+
+    all_of(po.at[0:10], s2, r2.at[0]).wait_recv()
+    for k, _ in chips[5:]:
+        back_slab(k).start()
+    all_of(po.at[0:5], s2, r2.at[1]).wait_recv()
+    for k, _ in chips[:5]:
+        back_slab(k).start()
 
     @pl.when(core == 1)
     def _():
@@ -492,7 +500,7 @@
     all_of(bhl.at[0 : NZ - 1], bhs, bhr).wait_send()
     all_of(dall.at[0 : NS - 1], dsend, drecv).wait_send()
     all_of(p1.at[0:15], s1, r1).wait_send()
-    all_of(po.at[0:15], s2, r2).wait_send()
+    all_of(po.at[0:15], s2, r2.at[0]).wait_send()
     across(early, 0).wait_send()
     back(late).wait_send()
 
@@ -579,7 +587,7 @@
         dma,
         dma,
         dma,
-        dma,
+        dma((2,)),
         dma,
         dma,
         dma((3,)),

time: 39.7 us -> 39.7 us (level)
  no operation moved by 1% of the time
where the time goes in v9:
time: 39.7 us
  Pallas kernels  39.6 us (100%)
    pallas_call x1, Pallas kernels, on_device(): pl.pallas_call(kernel, out_shape=(vmem((2, LEN, CI), BF16), vmem((8, 128)...  38.4 us
    pallas_call x1, Pallas kernels, on_device(): pl.pallas_call(scaled, out_shape=jax.ShapeDtypeStruct((2, LEN, CI), BF16)...  1.24 us

profile of v9, /device:TPU:1, one launch (start us, length us, event | category | flops | bytes accessed | tf_op | source)
XLA Modules:
  0.0 39.7 jit_solution(2080913840110805738)
XLA Ops:
  0.0 38.4 %shard_map.100 = (bf16[2,512,640]{2,1,0:T(8,128)(2,1)S(1)}, f32[8,128]{1,0:T(8,128)S(1)}) custom-call(bf16[2,512,2560]{2,1,0:T(8,128)(2,1)} %hid.1, bf16[2560,640]{1,0:T(8,128)(2,1)} %gw.1, bf16[2560,640]{1,0:T(8,128)(2,1)} %vw.1, bf16[32,2560]{1,0:T(8,128)(2,1)} %bitcast.4, bf16[10,2560]{1,0:T(8,128)(2,1)} %bitcast.5, f32[4,640]{1,0:T(4,128)} %vconv.1, ...), custom_call_target="tpu_custom_call" | custom-call | tf_op jit(solution)/shard_map/pallas_call | solution.py:597
  38.4 1.2 %shard_map.101 = bf16[2,512,640]{2,1,0:T(8,128)(2,1)} custom-call(bf16[2,512,640]{2,1,0:T(8,128)(2,1)S(1)} %get-tuple-element.7.gated, f32[8,128]{1,0:T(8,128)S(1)} %get-tuple-element.8.rms), custom_call_target="tpu_custom_call" | custom-call | tf_op jit(solution)/shard_map/pallas_call | solution.py:610
